TPU v7x, 128 devices: a whole 4x4x4 slice. The times are simulated.
128 devices in a mesh: ep: 64 (over z, y, x), dp: 2 (over core).
Axes of the slice: x: 4, y: 4, z: 4, core: 2. Of those that a mesh axis runs over, the one named last changes fastest.
Arguments:
- tokens: bfloat16 [32768, 448], P(('dp', 'ep'))
- d_out: bfloat16 [32768, 448], P(('dp', 'ep'))
- expert_ids: int32 [2, 32768, 8], P(None, ('dp', 'ep'))
- gate_vals: float32 [2, 32768, 8], P(None, ('dp', 'ep'))
- w_mix: bfloat16 [2, 448, 448], replicated
- w_gate: bfloat16 [2, 256, 448, 128], P(None, 'ep')
- w_up: bfloat16 [2, 256, 448, 128], P(None, 'ep')
- w_down: bfloat16 [2, 256, 128, 448], P(None, 'ep')
Outputs:
- output 1: bfloat16 [32768, 448], P(('dp', 'ep'))
- output 2: bfloat16 [32768, 448], P(('dp', 'ep'))
- output 3: bfloat16 [2, 448, 448], replicated
- output 4: bfloat16 [2, 256, 448, 128], P(None, 'ep')
- output 5: bfloat16 [2, 256, 448, 128], P(None, 'ep')
- output 6: bfloat16 [2, 256, 128, 448], P(None, 'ep')
All inputs are finite; a program needn't handle non-finite values.
Results may differ from a plain program's by a relative error of at most 0.02.
Values are sent between devices in bfloat16 or wider.
A program may use at most 1 GiB of HBM per device.

v0:
```python
import functools
import jax
import jax.numpy as jnp
from jax import lax
from jax.experimental import pallas as pl
from jax.experimental.pallas import tpu as pltpu
from jax.sharding import Mesh, PartitionSpec as P


F32 = jnp.float32
BF16 = jnp.bfloat16
MESH = pl.DeviceIdType.MESH
VMEM = pl.BlockSpec(memory_space=pltpu.VMEM)
COST = pl.CostEstimate(flops=8 * 10**9, bytes_accessed=10**7, transcendentals=0)


def enter(peers):
    barrier = pltpu.get_barrier_semaphore()
    for peer in peers:
        pl.semaphore_signal(barrier, inc=1, device_id=peer, device_id_type=MESH)
    pl.semaphore_wait(barrier, len(peers))


def send(src, dst, send_sems, recv_sems, index, peer):
    copy = pltpu.make_async_remote_copy(src_ref=src, dst_ref=dst, send_sem=send_sems.at[index],
                                        recv_sem=recv_sems.at[index], device_id=peer, device_id_type=MESH)
    copy.start()
    return copy


def line_peers():
    z, dp = lax.axis_index('z'), lax.axis_index('dp')
    up, down = {'z': lax.rem(z + 1, 4)}, {'z': lax.rem(z + 3, 4)}
    return z, dp, up, down, {'dp': 1 - dp}


N_AG = 9


def line_gather(src, dst, send_sems, recv_sems, base):
    z, dp, up, down, mate = line_peers()
    rows = src.shape[0]
    half = rows // 2
    me = z * 2 + dp
    below, above = lax.rem(z + 3, 4) * 2 + dp, lax.rem(z + 1, 4) * 2 + dp
    far = lax.rem(z + 2, 4) * 2 + dp
    lo, hi = pl.ds(0, half), pl.ds(half, half)
    go = functools.partial(send, send_sems=send_sems, recv_sems=recv_sems)
    to_up = go(src, dst.at[me], index=base, peer=up)
    to_down = go(src, dst.at[me], index=base + 1, peer=down)
    to_mate = go(src, dst.at[me], index=base + 2, peer=mate)
    dst[me] = src[...]
    to_up.wait_recv()
    relay_up = go(dst.at[below, lo], dst.at[below, lo], index=base + 3, peer=up)
    mate_below = go(dst.at[below], dst.at[below], index=base + 5, peer=mate)
    to_down.wait_recv()
    relay_down = go(dst.at[above, hi], dst.at[above, hi], index=base + 4, peer=down)
    mate_above = go(dst.at[above], dst.at[above], index=base + 6, peer=mate)
    relay_up.wait_recv()
    mate_lo = go(dst.at[far, lo], dst.at[far, lo], index=base + 7, peer=mate)
    relay_down.wait_recv()
    mate_hi = go(dst.at[far, hi], dst.at[far, hi], index=base + 8, peer=mate)
    for copy in (to_mate, mate_below, mate_above, mate_lo, mate_hi):
        copy.wait_recv()
    for copy in (to_up, to_down, to_mate, relay_up, relay_down, mate_below, mate_above, mate_lo, mate_hi):
        copy.wait_send()


N_RS = 10


def line_reduce(part, d_part, sums, relay_lo, relay_hi, in_lo, in_hi, send_sems, recv_sems, base):
    z, dp, up, down, mate = line_peers()
    half = part.shape[1] // 2
    lo, hi = pl.ds(0, half), pl.ds(half, half)
    order = [lax.rem(z + 2, 4), lax.rem(z + 1, 4), lax.rem(z + 3, 4), z]
    go = functools.partial(send, send_sems=send_sems, recv_sems=recv_sems)
    swaps = [go(part.at[zk * 2 + 1 - dp], d_part.at[k], index=base + k, peer=mate) for k, zk in enumerate(order)]
    swaps[0].wait_recv()
    sums[0] = part[order[0] * 2 + dp] + d_part[0]
    far_up = go(sums.at[0, lo], relay_lo, index=base + 4, peer=up)
    far_down = go(sums.at[0, hi], relay_hi, index=base + 5, peer=down)
    swaps[1].wait_recv()
    sums[1] = part[order[1] * 2 + dp] + d_part[1]
    up_hi = go(sums.at[1, hi], in_lo.at[hi], index=base + 6, peer=up)
    swaps[2].wait_recv()
    sums[2] = part[order[2] * 2 + dp] + d_part[2]
    down_lo = go(sums.at[2, lo], in_hi.at[lo], index=base + 7, peer=down)
    swaps[3].wait_recv()
    sums[3] = part[order[3] * 2 + dp] + d_part[3]
    far_up.wait_recv()
    sums[1, lo] = sums[1, lo] + relay_lo[...]
    up_lo = go(sums.at[1, lo], in_lo.at[lo], index=base + 8, peer=up)
    far_down.wait_recv()
    sums[2, hi] = sums[2, hi] + relay_hi[...]
    down_hi = go(sums.at[2, hi], in_hi.at[hi], index=base + 9, peer=down)
    up_hi.wait_recv()
    down_lo.wait_recv()
    up_lo.wait_recv()
    down_hi.wait_recv()
    for copy in swaps + [far_up, far_down, up_hi, down_lo, up_lo, down_hi]:
        copy.wait_send()
    return sums[3] + in_lo[...] + in_hi[...]


def reduce_scratch(tok, width):
    return [pltpu.VMEM((4, tok, width), F32), pltpu.VMEM((4, tok, width), F32),
            pltpu.VMEM((tok // 2, width), F32), pltpu.VMEM((tok // 2, width), F32),
            pltpu.VMEM((tok, width), F32), pltpu.VMEM((tok, width), F32)]


def params(collective_id):
    return pltpu.CompilerParams(collective_id=collective_id, has_side_effects=True,
                                vmem_limit_bytes=60 * 1024 * 1024)


def gather_kernel(src, dst, send_sems, recv_sems):
    _, _, up, down, mate = line_peers()
    enter((up, down, mate))
    line_gather(src, dst, send_sems, recv_sems, 0)


def gather_line(val, collective_id):
    return pl.pallas_call(
        gather_kernel, name='gather_line',
        out_shape=jax.ShapeDtypeStruct((8,) + val.shape, val.dtype),
        in_specs=[VMEM], out_specs=VMEM,
        scratch_shapes=[pltpu.SemaphoreType.DMA((N_AG,)), pltpu.SemaphoreType.DMA((N_AG,))],
        compiler_params=params(collective_id))(val)


def pass_kernel(transpose, want_all, part, base, w_mix, y_ref, next_ref, *rest):
    if want_all:
        all_ref, rest = rest[0], rest[1:]
    bufs, (send_sems, recv_sems) = rest[:-2], rest[-2:]
    _, _, up, down, mate = line_peers()
    enter((up, down, mate))
    total = line_reduce(part, *bufs, send_sems, recv_sems, 0)
    y_val = (base[...].astype(F32) + total).astype(BF16)
    y_ref[...] = y_val
    contract = (((1,), (1 if transpose else 0,)), ((), ()))
    mixed = lax.dot_general(y_val, w_mix[...], contract, preferred_element_type=F32)
    next_ref[...] = (y_val.astype(F32) + mixed).astype(BF16)
    if want_all:
        line_gather(next_ref, all_ref, send_sems, recv_sems, N_RS)


def pass_line(part, base, w_mix, transpose, want_all, collective_id):
    _, tok, width = part.shape
    block = jax.ShapeDtypeStruct((tok, width), BF16)
    outs = [block, block] + ([jax.ShapeDtypeStruct((8, tok, width), BF16)] if want_all else [])
    n_sem = N_RS + (N_AG if want_all else 0)
    return pl.pallas_call(
        functools.partial(pass_kernel, transpose, want_all), name='pass_line',
        out_shape=outs, in_specs=[VMEM] * 3, out_specs=[VMEM] * len(outs),
        scratch_shapes=reduce_scratch(tok, width) + [pltpu.SemaphoreType.DMA((n_sem,)),
                                                     pltpu.SemaphoreType.DMA((n_sem,))],
        compiler_params=params(collective_id))(part, base, w_mix)


def finish_kernel(part, base, y_ref, *rest):
    bufs, (send_sems, recv_sems) = rest[:-2], rest[-2:]
    _, _, up, down, mate = line_peers()
    enter((up, down, mate))
    total = line_reduce(part, *bufs, send_sems, recv_sems, 0)
    y_ref[...] = (base[...].astype(F32) + total).astype(BF16)


def finish_line(part, base, collective_id):
    _, tok, width = part.shape
    return pl.pallas_call(
        finish_kernel, name='finish_line',
        out_shape=jax.ShapeDtypeStruct((tok, width), BF16), in_specs=[VMEM] * 2, out_specs=VMEM,
        scratch_shapes=reduce_scratch(tok, width) + [pltpu.SemaphoreType.DMA((N_RS,)),
                                                     pltpu.SemaphoreType.DMA((N_RS,))],
        compiler_params=params(collective_id))(part, base)


def mix_kernel(grad, out, mate_in, quarter_in, block, y_in, y_out, z_in, z_out, send_sems, recv_sems):
    dp = lax.axis_index('dp')
    mate = {'dp': 1 - dp}
    at = {axis: lax.axis_index(axis) for axis in 'xyz'}
    peers = {axis: [{axis: lax.rem(at[axis] + k, 4)} for k in (1, 2, 3)] for axis in 'xyz'}
    enter(peers['x'] + peers['y'] + peers['z'] + [mate])
    quarter = grad.shape[1] // 4
    go = functools.partial(send, send_sems=send_sems, recv_sems=recv_sems)
    copies = []
    swap = go(grad.at[1 - dp], mate_in, index=0, peer=mate)
    swap.wait_recv()
    block[...] = (grad[dp].astype(F32) + mate_in[...].astype(F32)).astype(BF16)
    mine = pl.ds(pl.multiple_of(at['x'] * quarter, quarter), quarter)
    stage = []
    for k in range(3):
        rows = pl.ds(pl.multiple_of(lax.rem(at['x'] + k + 1, 4) * quarter, quarter), quarter)
        stage.append(go(block.at[rows], quarter_in.at[k], index=1 + k, peer=peers['x'][k]))
    copies += [swap] + stage
    total = block[mine].astype(F32)
    for k in range(3):
        stage[k].wait_recv()
        total = total + quarter_in[k].astype(F32)
    for axis, buf_in, buf_out, base in (('y', y_in, y_out, 4), ('z', z_in, z_out, 7)):
        buf_out[...] = total.astype(BF16)
        stage = [go(buf_out, buf_in.at[k], index=base + k, peer=peers[axis][k]) for k in range(3)]
        copies += stage
        terms = [buf_out[...].astype(F32)]
        for k in range(3):
            stage[k].wait_recv()
            terms.append(buf_in[k].astype(F32))
        here = at[axis]
        total = None
        for coord in range(4):
            term = jnp.zeros_like(terms[0])
            for k in range(4):
                source = lax.rem(here + 4 - k, 4)
                term = jnp.where(source == coord, terms[k], term)
            total = term if total is None else total + term
    final = total.astype(BF16)
    out[dp, mine] = final
    stage = [go(out.at[dp, mine], out.at[dp, mine], index=10 + k, peer=peers['x'][k]) for k in range(3)]
    copies += stage
    for k in range(3):
        stage[k].wait_recv()
    swap = go(out.at[dp], out.at[dp], index=13, peer=mate)
    swap.wait_recv()
    copies.append(swap)
    for copy in copies:
        copy.wait_send()


def mix_sum(grad, collective_id):
    _, rows, width = grad.shape
    quarter = rows // 4
    return pl.pallas_call(
        mix_kernel, name='mix_sum',
        out_shape=jax.ShapeDtypeStruct(grad.shape, BF16), in_specs=[VMEM], out_specs=VMEM,
        scratch_shapes=[pltpu.VMEM((rows, width), BF16), pltpu.VMEM((3, quarter, width), BF16),
                        pltpu.VMEM((rows, width), BF16),
                        pltpu.VMEM((3, quarter, width), BF16), pltpu.VMEM((quarter, width), BF16),
                        pltpu.VMEM((3, quarter, width), BF16), pltpu.VMEM((quarter, width), BF16),
                        pltpu.SemaphoreType.DMA((14,)), pltpu.SemaphoreType.DMA((14,))],
        compiler_params=params(collective_id))(grad)


def silu_parts(pre_gate):
    sig_val = jax.nn.sigmoid(pre_gate)
    return pre_gate * sig_val, sig_val * (1.0 + pre_gate * (1.0 - sig_val))


def split3(val):
    hi = lax.reduce_precision(val, 8, 7)
    rest = val - hi
    mid = lax.reduce_precision(rest, 8, 7)
    return hi, mid, rest - mid


def dot(spec, a, b):
    return jnp.einsum(spec, a, b, preferred_element_type=F32)


CHUNK = 8
SLOT = 32


def pick(pos_row, slots):
    return jnp.broadcast_to(pos_row, slots.shape) == slots


def one_hot(pos, source, values=None):
    n_tok = pos.shape[2]
    slots = lax.broadcasted_iota(jnp.int32, (SLOT, n_tok), 0).astype(F32)
    blocks = []
    for e in range(CHUNK):
        mask = pick(pos[source, e:e + 1, :], slots)
        val = 1.0 if values is None else jnp.broadcast_to(values[source, e:e + 1, :], mask.shape)
        blocks.append(jnp.where(mask, val, 0.0))
    return jnp.concatenate(blocks, axis=0)


def nn(a, b):
    return lax.dot_general(a, b, (((1,), (0,)), ((), ())), preferred_element_type=F32)


def nt(a, b):
    return lax.dot_general(a, b, (((1,), (1,)), ((), ())), preferred_element_type=F32)


def tn(a, b):
    return lax.dot_general(a, b, (((0,), (0,)), ((), ())), preferred_element_type=F32)


def forward_kernel(pos, u_all, w_in, recv, pre_gate, pre_up, hidden):
    for s in range(8):
        rows = nn(one_hot(pos, s).astype(BF16), u_all[s]).astype(BF16)
        for e in range(CHUNK):
            recv[e, s * SLOT:(s + 1) * SLOT, :] = rows[e * SLOT:(e + 1) * SLOT]
    for e in range(CHUNK):
        w_both = jnp.concatenate([w_in[e // 2, 0, e % 2], w_in[e // 2, 1, e % 2]], axis=1)
        both = nn(recv[e], w_both)
        a, b = both[:, :128], both[:, 128:]
        act, _ = silu_parts(a)
        pre_gate[e] = a
        pre_up[e] = b
        hidden[e] = (act * b).astype(BF16)


def route_spec_of(n_tok):
    return pl.BlockSpec((8, CHUNK, n_tok), lambda i: (0, i, 0))


def local_params():
    return pltpu.CompilerParams(vmem_limit_bytes=60 * 1024 * 1024)


def expert_forward(pos, u_all, weights):
    _, n_mine, n_tok = pos.shape
    width = u_all.shape[2]
    ff = weights.shape[4]
    rows = 8 * SLOT
    per = lambda last: pl.BlockSpec((CHUNK, rows, last), lambda i: (i, 0, 0))
    return pl.pallas_call(
        forward_kernel, name='expert_forward', grid=(n_mine // CHUNK,),
        out_shape=[jax.ShapeDtypeStruct((n_mine, rows, width), BF16),
                   jax.ShapeDtypeStruct((n_mine, rows, ff), F32),
                   jax.ShapeDtypeStruct((n_mine, rows, ff), F32),
                   jax.ShapeDtypeStruct((n_mine, rows, ff), BF16)],
        in_specs=[route_spec_of(n_tok), pl.BlockSpec(u_all.shape, lambda i: (0, 0, 0)),
                  pl.BlockSpec((CHUNK // 2, 2, 2, width, ff), lambda i: (i, 0, 0, 0, 0))],
        out_specs=[per(width), per(ff), per(ff), per(ff)],
        compiler_params=local_params())(pos, u_all, weights)


def combine_kernel(n_left, pos, hi, mid, lo, *refs):
    lefts, w_out, part, rows = refs[:n_left], refs[n_left], refs[n_left + 1], refs[n_left + 2]
    for e in range(CHUNK):
        left = jnp.concatenate([ref[e] for ref in lefts], axis=1)
        right = jnp.concatenate([w_out[e // 2, k, e % 2] for k in range(n_left)], axis=1)
        rows[e] = nt(left, right).astype(BF16)
    for s in range(8):
        mine = jnp.concatenate([rows[e, s * SLOT:(s + 1) * SLOT, :] for e in range(CHUNK)], axis=0)
        val = tn(one_hot(pos, s, lo).astype(BF16), mine)
        val = val + tn(one_hot(pos, s, mid).astype(BF16), mine)
        val = val + tn(one_hot(pos, s, hi).astype(BF16), mine)

        @pl.when(pl.program_id(0) == 0)
        def _(val=val, s=s):
            part[s] = val

        @pl.when(pl.program_id(0) > 0)
        def _(val=val, s=s):
            part[s] = part[s] + val


def expert_combine(pos, gate_parts, lefts, weights, which):
    _, n_mine, n_tok = pos.shape
    width, ff = weights.shape[3:]
    rows = 8 * SLOT
    n_left = len(lefts)
    per = pl.BlockSpec((CHUNK, rows, ff), lambda i: (i, 0, 0))
    return pl.pallas_call(
        functools.partial(combine_kernel, n_left), name='expert_combine', grid=(n_mine // CHUNK,),
        out_shape=jax.ShapeDtypeStruct((8, n_tok, width), F32),
        in_specs=[route_spec_of(n_tok)] * 4 + [per] * n_left
        + [pl.BlockSpec((CHUNK // 2, n_left, 2, width, ff), lambda i: (i, which // n_left, 0, 0, 0))],
        out_specs=pl.BlockSpec((8, n_tok, width), lambda i: (0, 0, 0)),
        scratch_shapes=[pltpu.VMEM((CHUNK, rows, width), BF16)],
        compiler_params=local_params())(pos, *gate_parts, *lefts, weights)


def backward_kernel(pos, gate, dy_all, w_out, recv, pre_gate, pre_up, hidden, pack, d_gate, d_up, grad_in):
    for s in range(8):
        sel = one_hot(pos, s).astype(BF16)
        gate_slot = jnp.sum(one_hot(pos, s, gate), axis=1, keepdims=True)
        rows = (gate_slot * nn(sel, dy_all[s])).astype(BF16)
        for e in range(CHUNK):
            grad_in[e, s * SLOT:(s + 1) * SLOT, :] = rows[e * SLOT:(e + 1) * SLOT]
    for e in range(CHUNK):
        c = grad_in[e]
        d_hidden = nn(c, w_out[e // 2, 0, e % 2])
        act, slope = silu_parts(pre_gate[e])
        da = (d_hidden * pre_up[e] * slope).astype(BF16)
        db = (d_hidden * act).astype(BF16)
        d_gate[e] = da
        d_up[e] = db
        both = tn(recv[e], jnp.concatenate([da, db], axis=1)).astype(BF16)
        pack[e // 2, 0, e % 2] = both[:, :128]
        pack[e // 2, 1, e % 2] = both[:, 128:]
        pack[e // 2, 2, e % 2] = tn(c, hidden[e]).astype(BF16)


def expert_backward(pos, gate, dy_all, weights, recv, pre_gate, pre_up, hidden):
    _, n_mine, n_tok = pos.shape
    width, ff = weights.shape[3:]
    rows = 8 * SLOT
    per = lambda last: pl.BlockSpec((CHUNK, rows, last), lambda i: (i, 0, 0))
    return pl.pallas_call(
        backward_kernel, name='expert_backward', grid=(n_mine // CHUNK,),
        out_shape=[jax.ShapeDtypeStruct(weights.shape, BF16),
                   jax.ShapeDtypeStruct((n_mine, rows, ff), BF16),
                   jax.ShapeDtypeStruct((n_mine, rows, ff), BF16)],
        in_specs=[route_spec_of(n_tok)] * 2 + [pl.BlockSpec(dy_all.shape, lambda i: (0, 0, 0)),
                  pl.BlockSpec((CHUNK // 2, 1, 2, width, ff), lambda i: (i, 2, 0, 0, 0)),
                  per(width), per(ff), per(ff), per(ff)],
        out_specs=[pl.BlockSpec((CHUNK // 2, 3, 2, width, ff), lambda i: (i, 0, 0, 0, 0)), per(ff), per(ff)],
        scratch_shapes=[pltpu.VMEM((CHUNK, rows, width), BF16)],
        compiler_params=local_params())(pos, gate, dy_all, weights, recv, pre_gate, pre_up, hidden)


def routing(ids, gates, my_experts):
    hit = ids[:, None, :, :] == my_experts[None, :, None, None]
    used = jnp.any(hit, axis=3)
    gate_et = jnp.sum(jnp.where(hit, gates[:, None, :, :], 0.0), axis=3)
    n_tok = ids.shape[1]
    row = lax.broadcasted_iota(jnp.int32, (n_tok, n_tok), 0)
    col = lax.broadcasted_iota(jnp.int32, (n_tok, n_tok), 1)
    pos = dot('sit,tu->siu', used.astype(BF16), (row < col).astype(BF16))
    return jnp.where(used, pos, -1.0), gate_et


def solution(mesh):
    m4 = Mesh(mesh.devices.reshape(4, 4, 4, 2), ('z', 'y', 'x', 'dp'))
    ep = ('z', 'y', 'x')
    tok_spec = P(('dp',) + ep, None)
    route_spec = P(None, ('dp',) + ep, None)
    whole_spec = P(None, None, None)
    expert_spec = P(None, ep, None, None)

    def device_body(tokens, d_out, expert_ids, gate_vals, w_mix, w_gate, w_up, w_down):
        n_layers = w_mix.shape[0]
        n_chip = w_gate.shape[1]
        n_half = n_chip // 2
        tok_local, d_model = tokens.shape
        ff = w_gate.shape[3]
        top_k = expert_ids.shape[2]
        dp = lax.axis_index('dp')
        zi = lax.axis_index('z')
        n_mine = 16 * n_half
        loc = jnp.arange(n_mine, dtype=jnp.int32)
        my_experts = (zi * 16 + loc // n_half) * n_chip + dp * n_half + loc % n_half

        def gather_weights(layer):
            wg = lax.dynamic_slice_in_dim(w_gate[layer], dp * n_half, n_half, 0)
            wu = lax.dynamic_slice_in_dim(w_up[layer], dp * n_half, n_half, 0)
            wd = lax.dynamic_slice_in_dim(w_down[layer], dp * n_half, n_half, 0)
            pack = jnp.stack([wg, wu, jnp.swapaxes(wd, 1, 2)], axis=0)
            pack = pack.reshape(3 * n_half * d_model, ff)
            full = lax.all_gather(pack, ('y', 'x'), axis=0, tiled=False)
            return full.reshape(16, 3, n_half, d_model, ff)

        def scatter_grads(pack):
            part = lax.psum_scatter(pack.reshape(16 * 3 * n_half * d_model, ff), ('y', 'x'),
                                    scatter_dimension=0, tiled=True)
            return part

        def finish_grads(part):
            other = lax.ppermute(part, 'dp', [(0, 1), (1, 0)])
            lo = jnp.where(dp == 0, part, other).reshape(3, n_half, d_model, ff)
            hi = jnp.where(dp == 0, other, part).reshape(3, n_half, d_model, ff)
            both = jnp.concatenate([lo, hi], axis=1)
            return both[0], both[1], jnp.swapaxes(both[2], 1, 2)

        weights = [gather_weights(layer) for layer in range(n_layers)]

        route_pack = []
        for layer in range(n_layers):
            route_pack.append(expert_ids[layer].astype(BF16))
            route_pack.extend(part.astype(BF16) for part in split3(gate_vals[layer]))
        route_pack = jnp.concatenate(route_pack, axis=1)

        u_act = (tokens.astype(F32) + dot('td,de->te', tokens, w_mix[0])).astype(BF16)
        pad = route_pack.shape[1]
        first = jnp.concatenate([jnp.concatenate([u_act, route_pack], axis=1),
                                 jnp.pad(d_out, ((0, 0), (0, pad)))], axis=0)
        got = gather_line(first, 1)
        u_all = got[:, :tok_local, :d_model]
        dy_all = got[:, tok_local:, :d_model]
        r_all = got[:, :tok_local, d_model:]
        routes = []
        for layer in range(n_layers):
            seg = r_all[:, :, layer * 4 * top_k:(layer + 1) * 4 * top_k]
            ids = seg[:, :, :top_k].astype(jnp.int32)
            gates = (seg[:, :, top_k:2 * top_k].astype(F32) + seg[:, :, 2 * top_k:3 * top_k].astype(F32)
                     + seg[:, :, 3 * top_k:].astype(F32))
            pos, gate = routing(ids, gates, my_experts)
            routes.append((pos, gate, split3(gate)))

        layer_in = tokens
        saved = []
        for layer in range(n_layers):
            pos, gate, parts = routes[layer]
            if layer > 0:
                weights[layer], u_all = lax.optimization_barrier((weights[layer], u_all))
            state = expert_forward(pos, u_all, weights[layer])
            saved.append((layer_in, u_act, state))
            if layer < n_layers - 1:
                part = expert_combine(pos, parts, state[3:], weights[layer], 2)
                layer_in, u_act, u_all = pass_line(part, u_act, w_mix[layer + 1], False, True, 2 + layer)

        d_y = d_out
        mix_grads = []
        grads = []
        for layer in reversed(range(n_layers)):
            x_in, u_act, state = saved[layer]
            pos, gate, parts = routes[layer]
            pack, d_gate, d_up = expert_backward(pos, gate, dy_all, weights[layer], *state)
            grads.insert(0, scatter_grads(pack))
            part = expert_combine(pos, parts, (d_gate, d_up), weights[layer], 0)
            if layer > 0:
                d_u, d_y, dy_all = pass_line(part, d_y, w_mix[layer], True, True, 4 + layer)
            else:
                d_u, d_y = pass_line(part, d_y, w_mix[layer], True, False, 4)
            mix_grads.insert(0, dot('td,te->de', x_in, d_u).astype(BF16))
        x_in, u_act, state = saved[-1]
        pos, gate, parts = routes[-1]
        hidden, d_y = lax.optimization_barrier((state[3], d_y))
        layer_out = finish_line(expert_combine(pos, parts, (hidden,), weights[-1], 2), u_act, 6)
        mix_out = mix_sum(jnp.stack(mix_grads), 7)
        grads[1], layer_out = lax.optimization_barrier((grads[1], layer_out))
        grads = [finish_grads(part) for part in grads]
        return (layer_out, d_y, mix_out) + tuple(jnp.stack([g[k] for g in grads]) for k in range(3))

    return jax.shard_map(device_body, mesh=m4,
                         in_specs=(tok_spec, tok_spec, route_spec, route_spec, whole_spec,
                                   expert_spec, expert_spec, expert_spec),
                         out_specs=(tok_spec, tok_spec, whole_spec, expert_spec, expert_spec, expert_spec),
                         check_vma=False)
```

profile of v0, /device:TPU:1, one launch (start us, length us, event | category | flops | bytes accessed | tf_op | source)
XLA Modules:
  0.0 540.5 jit_solution(7396450788324349721)
XLA Ops:
  13.7 29.4 %gather_line.1 = bf16[8,512,512]{2,1,0:T(8,128)(2,1)} custom-call(bf16[512,512]{1,0:T(8,128)(2,1)} %fusion.6.src), custom_call_target="tpu_custom_call" | custom-call | tf_op jit(solution)/shard_map/gather_line/pallas_call | solution.py:124
  43.1 1.9 slice_convert_fusion.1
  45.6 4.0 convert_add_fusion.1
  50.2 1.7 compare_reduce_fusion
  51.9 1.4 fusion.1
  58.1 2.3 fusion.22
  60.4 35.8 %all-gather.5.cloned.1.call-done = bf16[16,2688,128]{2,1,0:T(8,128)(2,1)} async-done(((bf16[1,2688,128]{2,1,0:T(8,128)(2,1)}), bf16[16,2688,128]{2,1,0:T(8,128)(2,1)}) %all-gather.5.cloned.1.call-update) | async-done | bytes 11010064 | tf_op jit(solution)/shard_map/all_gather | solution.py:446
  96.3 11.2 %expert_forward.2 = (bf16[32,256,448]{2,1,0:T(8,128)(2,1)}, f32[32,256,128]{2,1,0:T(8,128)}, f32[32,256,128]{2,1,0:T(8,128)}, bf16[32,256,128]{2,1,0:T(8,128)(2,1)}) custom-call(f32[8,32,256]{2,1,0:T(8,128)} %convolution_select_fusion.pos, bf16[8,256,448]{2,1,0:T(8,128)(2,1)} %get-tuple-element.90.u_all, bf16[16,3,2,448,128]{4,3,2,1,0:T(8,128)(2,1)} %bitcast.74), custom_call_target="tpu_custom_call" | custom-call | tf_op jit(solution)/shard_map/expert_forward/pallas_call | solution.py:320
  107.5 20.4 %expert_combine.4.part = f32[8,256,448]{2,1,0:T(8,128)} custom-call(f32[8,32,256]{2,1,0:T(8,128)} %convolution_select_fusion.pos, f32[8,32,256]{2,1,0:T(8,128)} %get-tuple-element.119.hi, f32[8,32,256]{2,1,0:T(8,128)} %get-tuple-element.118.mid, f32[8,32,256]{2,1,0:T(8,128)} %get-tuple-element.117.lo, ...), custom_call_target="tpu_custom_call" | custom-call | tf_op jit(solution)/shard_map/expert_combine/pallas_call | solution.py:359
  127.8 41.9 %pass_line.3 = (bf16[256,448]{1,0:T(8,128)(2,1)}, bf16[256,448]{1,0:T(8,128)(2,1)}, bf16[8,256,448]{2,1,0:T(8,128)(2,1)}) custom-call(f32[8,256,448]{2,1,0:T(8,128)} %expert_combine.4.part, bf16[256,448]{1,0:T(8,128)(2,1)} %copy-done.5, bf16[448,448]{1,0:T(8,128)(2,1)} %get-tuple-element.107.w_mix), custom_call_target="tpu_custom_call" | custom-call | tf_op jit(solution)/shard_map/pass_line/pallas_call | solution.py:153
  169.7 11.5 %all-gather.3.cloned.1.call-done = bf16[16,2688,128]{2,1,0:T(8,128)(2,1)} async-done(((bf16[1,2688,128]{2,1,0:T(8,128)(2,1)}), bf16[16,2688,128]{2,1,0:T(8,128)(2,1)}) %all-gather.3.cloned.1.call-update) | async-done | bytes 11010064 | tf_op jit(solution)/shard_map/all_gather | solution.py:446
  181.2 11.2 %expert_forward.3 = (bf16[32,256,448]{2,1,0:T(8,128)(2,1)}, f32[32,256,128]{2,1,0:T(8,128)}, f32[32,256,128]{2,1,0:T(8,128)}, bf16[32,256,128]{2,1,0:T(8,128)(2,1)}) custom-call(f32[8,32,256]{2,1,0:T(8,128)} %convolution_select_fusion.1.pos, bf16[8,256,448]{2,1,0:T(8,128)(2,1)} %get-tuple-element.37.u_all, bf16[16,3,2,448,128]{4,3,2,1,0:T(8,128)(2,1)} %bitcast.78), custom_call_target="tpu_custom_call" | custom-call | tf_op jit(solution)/shard_map/expert_forward/pallas_call | solution.py:320
  192.5 18.7 %expert_backward.2 = (bf16[16,3,2,448,128]{4,3,2,1,0:T(8,128)(2,1)}, bf16[32,256,128]{2,1,0:T(8,128)(2,1)}, bf16[32,256,128]{2,1,0:T(8,128)(2,1)}) custom-call(f32[8,32,256]{2,1,0:T(8,128)} %convolution_select_fusion.1.pos, f32[8,32,256]{2,1,0:T(8,128)} %copy-done.3, bf16[8,256,448]{2,1,0:T(8,128)(2,1)} %get-tuple-element.91.dy_all, ...), custom_call_target="tpu_custom_call" | custom-call | tf_op jit(solution)/shard_map/expert_backward/pallas_call | solution.py:395
  211.2 21.1 %expert_combine.5.part = f32[8,256,448]{2,1,0:T(8,128)} custom-call(f32[8,32,256]{2,1,0:T(8,128)} %convolution_select_fusion.1.pos, f32[8,32,256]{2,1,0:T(8,128)} %get-tuple-element.116.hi, f32[8,32,256]{2,1,0:T(8,128)} %get-tuple-element.115.mid, f32[8,32,256]{2,1,0:T(8,128)} %get-tuple-element.114.lo, bf16[32,256,128]{2,1,0:T(8,128)(2,1)} %get-tuple-element.43.refs_0_, ...), custom_call_target="tpu_custom_call" | custom-call | tf_op jit(solution)/shard_map/expert_combine/pallas_call | solution.py:359
  232.3 41.5 %pass_line.4 = (bf16[256,448]{1,0:T(8,128)(2,1)}, bf16[256,448]{1,0:T(8,128)(2,1)}, bf16[8,256,448]{2,1,0:T(8,128)(2,1)}) custom-call(f32[8,256,448]{2,1,0:T(8,128)} %expert_combine.5.part, bf16[256,448]{1,0:T(8,128)(2,1)} %copy-done.4, bf16[448,448]{1,0:T(8,128)(2,1)} %get-tuple-element.107.w_mix), custom_call_target="tpu_custom_call" | custom-call | tf_op jit(solution)/shard_map/pass_line/pallas_call | solution.py:153
  273.8 18.8 %expert_backward.3 = (bf16[16,3,2,448,128]{4,3,2,1,0:T(8,128)(2,1)}, bf16[32,256,128]{2,1,0:T(8,128)(2,1)}, bf16[32,256,128]{2,1,0:T(8,128)(2,1)}) custom-call(f32[8,32,256]{2,1,0:T(8,128)} %convolution_select_fusion.pos, f32[8,32,256]{2,1,0:T(8,128)} %copy-done.2, bf16[8,256,448]{2,1,0:T(8,128)(2,1)} %get-tuple-element.45.dy_all, ...), custom_call_target="tpu_custom_call" | custom-call | tf_op jit(solution)/shard_map/expert_backward/pallas_call | solution.py:395
  293.1 89.3 %reduce-scatter.5.cloned.1.call-done = bf16[2688,128]{1,0:T(8,128)(2,1)} async-done(((bf16[43008,128]{1,0:T(8,128)(2,1)}), bf16[2688,128]{1,0:T(8,128)(2,1)}) %reduce-scatter.5.cloned.1.call-update) | async-done | bytes 688144 | tf_op jit(solution)/shard_map/reduce_scatter | solution.py:450
  382.4 1.7 collective-permute-start
  384.1 20.8 %expert_combine.6.part = f32[8,256,448]{2,1,0:T(8,128)} custom-call(f32[8,32,256]{2,1,0:T(8,128)} %convolution_select_fusion.pos, f32[8,32,256]{2,1,0:T(8,128)} %get-tuple-element.119.hi, f32[8,32,256]{2,1,0:T(8,128)} %get-tuple-element.118.mid, f32[8,32,256]{2,1,0:T(8,128)} %get-tuple-element.117.lo, bf16[32,256,128]{2,1,0:T(8,128)(2,1)} %get-tuple-element.49.refs_0_, ...), custom_call_target="tpu_custom_call" | custom-call | tf_op jit(solution)/shard_map/expert_combine/pallas_call | solution.py:359
  404.9 26.3 %pass_line.5 = (bf16[256,448]{1,0:T(8,128)(2,1)}, bf16[256,448]{1,0:T(8,128)(2,1)}) custom-call(f32[8,256,448]{2,1,0:T(8,128)} %expert_combine.6.part, bf16[256,448]{1,0:T(8,128)(2,1)} %get-tuple-element.51.base, bf16[448,448]{1,0:T(8,128)(2,1)} %get-tuple-element.106.w_mix), custom_call_target="tpu_custom_call" | custom-call | tf_op jit(solution)/shard_map/pass_line/pallas_call | solution.py:153
  431.3 20.4 %expert_combine.7.part = f32[8,256,448]{2,1,0:T(8,128)} custom-call(f32[8,32,256]{2,1,0:T(8,128)} %convolution_select_fusion.1.pos, f32[8,32,256]{2,1,0:T(8,128)} %get-tuple-element.116.hi, f32[8,32,256]{2,1,0:T(8,128)} %get-tuple-element.115.mid, f32[8,32,256]{2,1,0:T(8,128)} %get-tuple-element.114.lo, ...), custom_call_target="tpu_custom_call" | custom-call | tf_op jit(solution)/shard_map/expert_combine/pallas_call | solution.py:359
  453.4 46.2 %mix_sum.1 = bf16[2,448,448]{2,1,0:T(8,128)(2,1)} custom-call(bf16[2,448,448]{2,1,0:T(8,128)(2,1)} %pad_maximum_fusion.grad), custom_call_target="tpu_custom_call" | custom-call | tf_op jit(solution)/shard_map/mix_sum/pallas_call | solution.py:233
  500.4 25.7 %finish_line.1 = bf16[256,448]{1,0:T(8,128)(2,1)} custom-call(f32[8,256,448]{2,1,0:T(8,128)} %expert_combine.7.part, bf16[256,448]{1,0:T(8,128)(2,1)} %get-tuple-element.54.base), custom_call_target="tpu_custom_call" | custom-call | tf_op jit(solution)/shard_map/finish_line/pallas_call | solution.py:171
  526.9 1.8 copy.60
  (94 shorter events, 21.4 us)
Async XLA Ops:
  7.2 89.1 %all-gather.5.cloned.1.call-start = ((), (), s32[]{:S(2)}) async-start(), calls=%async_computation.3 | async-start | bytes 11698176 | tf_op jit(solution)/shard_map/all_gather | solution.py:446
  7.2 1.5 copy-start.9
  7.2 1.7 copy-start.10
  10.0 1.4 copy-start.7
  10.1 1.6 copy-start.18
  10.1 171.2 %all-gather.3.cloned.1.call-start = ((), (), s32[]{:S(2)}) async-start(), calls=%async_computation.2 | async-start | bytes 11698176 | tf_op jit(solution)/shard_map/all_gather | solution.py:446
  10.2 1.6 copy-start.17
  11.1 1.2 copy-start.6
  11.1 371.2 %reduce-scatter.5.cloned.1.call-start = ((), (), s32[]{:S(2)}) async-start(), calls=%async_computation.5 | async-start | bytes 11698176 | tf_op jit(solution)/shard_map/reduce_scatter | solution.py:450
  12.0 1.8 copy-start.4
  12.6 30.5 %copy-start.5 = (bf16[256,448]{1,0:T(8,128)(2,1)}, bf16[256,448]{1,0:T(8,128)(2,1)S(1)}, u32[]{:S(2)}) copy-start(bf16[256,448]{1,0:T(8,128)(2,1)S(1)} %fusion.4.base) | copy-start | bytes 688132
  53.3 4.8 copy-start.2
  53.3 4.8 copy-start.3
  54.2 3.9 copy-start
  292.6 233.6 %reduce-scatter.3.cloned.1.call-start = ((), (), s32[]{:S(2)}) async-start(), calls=%async_computation.4 | async-start | bytes 11698176 | tf_op jit(solution)/shard_map/reduce_scatter | solution.py:450
  382.4 146.3 %collective-permute-start = (bf16[2688,128]{1,0:T(8,128)(2,1)}, bf16[2688,128]{1,0:T(8,128)(2,1)S(1)}, u32[]{:S(2)}, u32[]{:S(2)}) collective-permute-start(bf16[2688,128]{1,0:T(8,128)(2,1)} %reduce-scatter.5.cloned.1.call-done), channel_id=1, source_target_pairs={{0,1},{1,0},{2,3},{3,2},{4,5},{5,4},{6,7},{7,6},{8,9},{9,8},{10,11... | collective-permute-start | bytes 2064392 | tf_op jit(solution)/shard_map/ppermute | solution.py:455
  431.2 20.5 %copy-start.8 = (bf16[256,448]{0,1:T(8,128)(2,1)S(1)}, bf16[256,448]{0,1:T(8,128)(2,1)}, u32[]{:S(2)}) copy-start(bf16[256,448]{0,1:T(8,128)(2,1)} %param.8) | copy-start | bytes 688132
  431.2 20.5 %copy-start.16 = (bf16[256,448]{1,0:T(8,128)(2,1)S(1)}, bf16[256,448]{1,0:T(8,128)(2,1)}, u32[]{:S(2)}) copy-start(bf16[256,448]{1,0:T(8,128)(2,1)} %get-tuple-element.57) | copy-start | bytes 688132
  431.2 20.7 %copy-start.14 = (bf16[256,448]{1,0:T(8,128)(2,1)S(1)}, bf16[256,448]{1,0:T(8,128)(2,1)}, u32[]{:S(2)}) copy-start(bf16[256,448]{1,0:T(8,128)(2,1)} %get-tuple-element.58) | copy-start | bytes 688132
  431.3 20.7 %copy-start.15 = (bf16[256,448]{1,0:T(8,128)(2,1)S(1)}, bf16[256,448]{1,0:T(8,128)(2,1)}, u32[]{:S(2)}) copy-start(bf16[256,448]{1,0:T(8,128)(2,1)} %get-tuple-element.59) | copy-start | bytes 688132
  452.0 47.5 %copy-start.13 = (bf16[256,448]{1,0:T(8,128)(2,1)S(1)}, bf16[256,448]{1,0:T(8,128)(2,1)}, u32[]{:S(2)}) copy-start(bf16[256,448]{1,0:T(8,128)(2,1)} %get-tuple-element.81) | copy-start | bytes 688132
  500.4 28.3 %copy-start.12 = (bf16[2688,128]{1,0:T(8,128)(2,1)S(1)}, bf16[2688,128]{1,0:T(8,128)(2,1)}, u32[]{:S(2)}) copy-start(bf16[2688,128]{1,0:T(8,128)(2,1)} %reduce-scatter.5.cloned.1.call-done) | copy-start | bytes 2064388
  526.1 2.8 collective-permute-start.1
  531.0 2.0 copy-start.1
  (2 other events, 2.3 us)
Sparse Core Ops, SparseCore 0:
  10.7 85.5 all-gather.4
  99.0 82.2 all-gather.2
  292.7 89.6 reduce-scatter.4
  385.7 97.1 reduce-scatter.2
where the time goes:
time: 541 us; the launch traced here: 540 us
  Pallas kernels  354 us (65%)
  waiting for transfers between devices  137 us (25%)
  other arithmetic  18.2 us (3%)
  between operations  14.2 us (3%)
  local copies, waits for them, and re-layouts  12 us (2%)
    pallas_call x3, Pallas kernels, pass_line(): pl.pallas_call(functools.partial(pass_kernel, transpose, want_all), name=...  110 us
    reduce_scatter x2, waiting for transfers between devices, scatter_grads(): lax.psum_scatter(pack.reshape(16 * 3 * n_half * d_model, ff), ('y', 'x'),...  89.3 us
    pallas_call x4, Pallas kernels, expert_combine(): pl.pallas_call(functools.partial(combine_kernel, n_left), name='expert_co...  82.7 us
    all_gather x2, waiting for transfers between devices, gather_weights(): full = lax.all_gather(pack, ('y', 'x'), axis=0, tiled=False)  47.3 us
    pallas_call x1, Pallas kernels, mix_sum(): pl.pallas_call(mix_kernel, name='mix_sum', out_shape=jax.ShapeDtypeStruct...  46.2 us
    pallas_call x2, Pallas kernels, expert_backward(): pl.pallas_call(backward_kernel, name='expert_backward', grid=(n_mine // C...  37.5 us
    pallas_call x1, Pallas kernels, gather_line(): pl.pallas_call(gather_kernel, name='gather_line', out_shape=jax.ShapeDtyp...  29.4 us
    pallas_call x1, Pallas kernels, finish_line(): pl.pallas_call(finish_kernel, name='finish_line', out_shape=jax.ShapeDtyp...  25.7 us
  transfers between devices with their start and end apart: 6, of which 3 were waited for; matrix products, arithmetic and copies ran while one was open for 5% of the time, Pallas kernels for 45%

commit v1 on v0

v1 whole, which is shorter than its diff:
```python
import functools
import jax
import jax.numpy as jnp
from jax import lax
from jax.experimental import pallas as pl
from jax.experimental.pallas import tpu as pltpu
from jax.sharding import Mesh, PartitionSpec as P


F32 = jnp.float32
BF16 = jnp.bfloat16
MESH = pl.DeviceIdType.MESH
VMEM = pl.BlockSpec(memory_space=pltpu.VMEM)


def enter(peers):
    barrier = pltpu.get_barrier_semaphore()
    for peer in peers:
        pl.semaphore_signal(barrier, inc=1, device_id=peer, device_id_type=MESH)
    pl.semaphore_wait(barrier, len(peers))


def send(src, dst, send_sems, recv_sems, index, peer):
    copy = pltpu.make_async_remote_copy(src_ref=src, dst_ref=dst, send_sem=send_sems.at[index],
                                        recv_sem=recv_sems.at[index], device_id=peer, device_id_type=MESH)
    copy.start()
    return copy


def line_peers():
    z, dp = lax.axis_index('z'), lax.axis_index('dp')
    up, down = {'z': lax.rem(z + 1, 4)}, {'z': lax.rem(z + 3, 4)}
    return z, dp, up, down, {'dp': 1 - dp}


N_AG = 9


def line_gather(src, dst, send_sems, recv_sems, base):
    for _ in line_gather_steps(src, dst, send_sems, recv_sems, base):
        pass


def line_gather_steps(src, dst, send_sems, recv_sems, base):
    z, dp, up, down, mate = line_peers()
    rows = src.shape[0]
    half = rows // 2
    me = z * 2 + dp
    below, above = lax.rem(z + 3, 4) * 2 + dp, lax.rem(z + 1, 4) * 2 + dp
    far = lax.rem(z + 2, 4) * 2 + dp
    lo, hi = pl.ds(0, half), pl.ds(half, half)
    go = functools.partial(send, send_sems=send_sems, recv_sems=recv_sems)
    to_up = go(src, dst.at[me], index=base, peer=up)
    to_down = go(src, dst.at[me], index=base + 1, peer=down)
    to_mate = go(src, dst.at[me], index=base + 2, peer=mate)
    dst[me] = src[...]
    yield
    to_up.wait_recv()
    relay_up = go(dst.at[below, lo], dst.at[below, lo], index=base + 3, peer=up)
    mate_below = go(dst.at[below], dst.at[below], index=base + 5, peer=mate)
    to_down.wait_recv()
    relay_down = go(dst.at[above, hi], dst.at[above, hi], index=base + 4, peer=down)
    mate_above = go(dst.at[above], dst.at[above], index=base + 6, peer=mate)
    yield
    relay_up.wait_recv()
    mate_lo = go(dst.at[far, lo], dst.at[far, lo], index=base + 7, peer=mate)
    relay_down.wait_recv()
    mate_hi = go(dst.at[far, hi], dst.at[far, hi], index=base + 8, peer=mate)
    for copy in (to_mate, mate_below, mate_above, mate_lo, mate_hi):
        copy.wait_recv()
    for copy in (to_up, to_down, to_mate, relay_up, relay_down, mate_below, mate_above, mate_lo, mate_hi):
        copy.wait_send()


N_RS = 10


def line_reduce_steps(part, bufs, send_sems, recv_sems, base):
    d_part, sums, relay_lo, relay_hi, in_lo, in_hi = bufs
    z, dp, up, down, mate = line_peers()
    half = part.shape[1] // 2
    lo, hi = pl.ds(0, half), pl.ds(half, half)
    order = [lax.rem(z + 2, 4), lax.rem(z + 1, 4), lax.rem(z + 3, 4), z]
    go = functools.partial(send, send_sems=send_sems, recv_sems=recv_sems)
    swaps = [go(part.at[zk * 2 + 1 - dp], d_part.at[k], index=base + k, peer=mate) for k, zk in enumerate(order)]
    yield
    swaps[0].wait_recv()
    sums[0] = part[order[0] * 2 + dp] + d_part[0]
    far_up = go(sums.at[0, lo], relay_lo, index=base + 4, peer=up)
    far_down = go(sums.at[0, hi], relay_hi, index=base + 5, peer=down)
    swaps[1].wait_recv()
    sums[1] = part[order[1] * 2 + dp] + d_part[1]
    up_hi = go(sums.at[1, hi], in_lo.at[hi], index=base + 6, peer=up)
    swaps[2].wait_recv()
    sums[2] = part[order[2] * 2 + dp] + d_part[2]
    down_lo = go(sums.at[2, lo], in_hi.at[lo], index=base + 7, peer=down)
    swaps[3].wait_recv()
    sums[3] = part[order[3] * 2 + dp] + d_part[3]
    far_up.wait_recv()
    sums[1, lo] = sums[1, lo] + relay_lo[...]
    up_lo = go(sums.at[1, lo], in_lo.at[lo], index=base + 8, peer=up)
    far_down.wait_recv()
    sums[2, hi] = sums[2, hi] + relay_hi[...]
    down_hi = go(sums.at[2, hi], in_hi.at[hi], index=base + 9, peer=down)
    yield
    for copy in (up_hi, down_lo, up_lo, down_hi):
        copy.wait_recv()
    for copy in swaps + [far_up, far_down, up_hi, down_lo, up_lo, down_hi]:
        copy.wait_send()
    yield sums[3] + in_lo[...] + in_hi[...]


def line_reduce(part, bufs, send_sems, recv_sems, base):
    for total in line_reduce_steps(part, bufs, send_sems, recv_sems, base):
        pass
    return total


def reduce_scratch(tok, width):
    return [pltpu.VMEM((4, tok, width), F32), pltpu.VMEM((4, tok, width), F32),
            pltpu.VMEM((tok // 2, width), F32), pltpu.VMEM((tok // 2, width), F32),
            pltpu.VMEM((tok, width), F32), pltpu.VMEM((tok, width), F32)]


def params(collective_id):
    return pltpu.CompilerParams(collective_id=collective_id, has_side_effects=True,
                                vmem_limit_bytes=60 * 1024 * 1024)


def pass_kernel(transpose, want_all, part, base, w_mix, y_ref, next_ref, *rest):
    if want_all:
        all_ref, rest = rest[0], rest[1:]
    bufs, (send_sems, recv_sems) = rest[:-2], rest[-2:]
    _, _, up, down, mate = line_peers()
    enter((up, down, mate))
    total = line_reduce(part, bufs, send_sems, recv_sems, 0)
    y_val = (base[...].astype(F32) + total).astype(BF16)
    y_ref[...] = y_val
    contract = (((1,), (1 if transpose else 0,)), ((), ()))
    mixed = lax.dot_general(y_val, w_mix[...], contract, preferred_element_type=F32)
    next_ref[...] = (y_val.astype(F32) + mixed).astype(BF16)
    if want_all:
        line_gather(next_ref, all_ref, send_sems, recv_sems, N_RS)


def pass_line(part, base, w_mix, transpose, want_all, collective_id):
    _, tok, width = part.shape
    block = jax.ShapeDtypeStruct((tok, width), BF16)
    outs = [block, block] + ([jax.ShapeDtypeStruct((8, tok, width), BF16)] if want_all else [])
    n_sem = N_RS + (N_AG if want_all else 0)
    return pl.pallas_call(
        functools.partial(pass_kernel, transpose, want_all), name='pass_line',
        out_shape=outs, in_specs=[VMEM] * 3, out_specs=[VMEM] * len(outs),
        scratch_shapes=reduce_scratch(tok, width) + [pltpu.SemaphoreType.DMA((n_sem,)),
                                                     pltpu.SemaphoreType.DMA((n_sem,))],
        compiler_params=params(collective_id))(part, base, w_mix)


def mix_peers():
    at = {axis: lax.axis_index(axis) for axis in 'xyz'}
    return at, {axis: [{axis: lax.rem(at[axis] + k, 4)} for k in (1, 2, 3)] for axis in 'xyz'}


def mix_steps(grad, out, bufs, send_sems, recv_sems, base):
    dp = lax.axis_index('dp')
    mate = {'dp': 1 - dp}
    at, peers = mix_peers()
    mate_in, quarter_in, block, y_in, y_out, z_in, z_out = bufs
    quarter = grad.shape[1] // 4
    go = functools.partial(send, send_sems=send_sems, recv_sems=recv_sems)
    copies = []
    swap = go(grad.at[1 - dp], mate_in, index=base, peer=mate)
    yield
    swap.wait_recv()
    block[...] = (grad[dp].astype(F32) + mate_in[...].astype(F32)).astype(BF16)
    mine = pl.ds(pl.multiple_of(at['x'] * quarter, quarter), quarter)
    stage = []
    for k in range(3):
        rows = pl.ds(pl.multiple_of(lax.rem(at['x'] + k + 1, 4) * quarter, quarter), quarter)
        stage.append(go(block.at[rows], quarter_in.at[k], index=base + 1 + k, peer=peers['x'][k]))
    copies += [swap] + stage
    yield
    total = block[mine].astype(F32)
    for k in range(3):
        stage[k].wait_recv()
        total = total + quarter_in[k].astype(F32)
    for axis, buf_in, buf_out, first in (('y', y_in, y_out, base + 4), ('z', z_in, z_out, base + 7)):
        buf_out[...] = total.astype(BF16)
        stage = [go(buf_out, buf_in.at[k], index=first + k, peer=peers[axis][k]) for k in range(3)]
        copies += stage
        terms = [buf_out[...].astype(F32)]
        for k in range(3):
            stage[k].wait_recv()
            terms.append(buf_in[k].astype(F32))
        here = at[axis]
        total = None
        for coord in range(4):
            term = jnp.zeros_like(terms[0])
            for k in range(4):
                source = lax.rem(here + 4 - k, 4)
                term = jnp.where(source == coord, terms[k], term)
            total = term if total is None else total + term
    final = total.astype(BF16)
    out[dp, mine] = final
    stage = [go(out.at[dp, mine], out.at[dp, mine], index=base + 10 + k, peer=peers['x'][k]) for k in range(3)]
    copies += stage
    for k in range(3):
        stage[k].wait_recv()
    swap = go(out.at[dp], out.at[dp], index=base + 13, peer=mate)
    swap.wait_recv()
    copies.append(swap)
    for copy in copies:
        copy.wait_send()
    yield


N_MIX = 14


def close_kernel(part_v, base_v, w_mix, x_in, mix_top, part_y, base_y, dx_ref, y_ref, mix_ref, *scratch):
    bufs_v, bufs_y, bufs_m = scratch[:6], scratch[6:12], scratch[12:19]
    grad, send_sems, recv_sems = scratch[19:]
    _, _, _, _, mate = line_peers()
    _, peers = mix_peers()
    enter(peers['x'] + peers['y'] + peers['z'] + [mate])
    steps_v = line_reduce_steps(part_v, bufs_v, send_sems, recv_sems, 0)
    steps_y = line_reduce_steps(part_y, bufs_y, send_sems, recv_sems, N_RS)
    steps_m = mix_steps(grad, mix_ref, bufs_m, send_sems, recv_sems, 2 * N_RS)
    next(steps_v)
    next(steps_y)
    grad[1] = mix_top[...]
    next(steps_v)
    d_u = (base_v[...].astype(F32) + next(steps_v)).astype(BF16)
    grad[0] = tn(x_in[...], d_u).astype(BF16)
    next(steps_m)
    dx_ref[...] = (d_u.astype(F32) + nt(d_u, w_mix[...])).astype(BF16)
    next(steps_m)
    next(steps_y)
    next(steps_m)
    y_ref[...] = (base_y[...].astype(F32) + next(steps_y)).astype(BF16)


def close_line(part_v, base_v, w_mix, x_in, mix_top, part_y, base_y, collective_id):
    _, tok, width = part_v.shape
    quarter = width // 4
    n_sem = 2 * N_RS + N_MIX
    block = jax.ShapeDtypeStruct((tok, width), BF16)
    return pl.pallas_call(
        close_kernel, name='close_line',
        out_shape=[block, block, jax.ShapeDtypeStruct((2, width, width), BF16)],
        in_specs=[VMEM] * 7, out_specs=[VMEM] * 3,
        scratch_shapes=reduce_scratch(tok, width) * 2
        + [pltpu.VMEM((width, width), BF16), pltpu.VMEM((3, quarter, width), BF16), pltpu.VMEM((width, width), BF16)]
        + [pltpu.VMEM((3, quarter, width), BF16), pltpu.VMEM((quarter, width), BF16)] * 2
        + [pltpu.VMEM((2, width, width), BF16), pltpu.SemaphoreType.DMA((n_sem,)), pltpu.SemaphoreType.DMA((n_sem,))],
        compiler_params=params(collective_id))(part_v, base_v, w_mix, x_in, mix_top, part_y, base_y)


N_PLANE = 40


def plane_gather_steps(src, dst, send_sems, recv_sems, base):
    at = {axis: lax.axis_index(axis) for axis in 'xy'}
    rows = src.shape[2] // 2
    part = (pl.ds(0, rows), pl.ds(rows, rows))
    go = functools.partial(send, send_sems=send_sems, recv_sems=recv_sems)
    copies = []

    def block(half, i, j):
        dx, dy = (i, j) if half == 0 else (j, i)
        return lax.rem(at['y'] + dy + 4, 4) * 4 + lax.rem(at['x'] + dx + 4, 4)

    def peer(half, stage, step):
        axis = 'xy'[stage] if half == 0 else 'yx'[stage]
        return {axis: lax.rem(at[axis] + step + 4, 4)}

    counter = [base]

    def launch(half, stage, step, i, j, rows_of=None, own=False):
        b = block(half, i, j)
        to = dst.at[b, :, half] if rows_of is None else dst.at[b, :, half, part[rows_of]]
        copy = go(src.at[:, half] if own else to, to, index=counter[0], peer=peer(half, stage, step))
        counter[0] += 1
        copies.append(copy)
        return copy

    first, second, relay1, relay2 = {}, {}, {}, {}
    for half in (0, 1):
        for step in (1, -1):
            first[half, step] = launch(half, 0, step, 0, 0, own=True)
    for half in (0, 1):
        for step in (1, -1):
            second[half, 0, step] = launch(half, 1, step, 0, 0, own=True)
    dst[at['y'] * 4 + at['x']] = src[...]
    yield
    for step in (1, -1):
        for half in (0, 1):
            first[half, step].wait_recv()
            relay1[half, step] = launch(half, 0, step, -step, 0, rows_of=0 if step == 1 else 1)
            for out in (1, -1):
                second[half, -step, out] = launch(half, 1, out, -step, 0)
    yield

    def forward(i):
        for step in (1, -1):
            for half in (0, 1):
                second[half, i, step].wait_recv()
                relay2[half, i, step] = launch(half, 1, step, i, -step, rows_of=0 if step == 1 else 1)

    forward(0)
    for half in (0, 1):
        for step in (1, -1):
            relay1[half, step].wait_recv()
        for out in (1, -1):
            second[half, 2, out] = launch(half, 1, out, 2, 0)
    yield
    forward(-1)
    forward(1)
    forward(2)
    for copy in relay2.values():
        copy.wait_recv()
    for copy in copies:
        copy.wait_send()
    yield


def open_kernel(n_chip, tok_src, route_src, w_src, tok_all, route, w_all, route_all, send_sems, recv_sems):
    z, dp, up, down, mate = line_peers()
    at = {axis: lax.axis_index(axis) for axis in 'xy'}
    enter([up, down, mate] + [{axis: lax.rem(at[axis] + k, 4)} for axis in 'xy' for k in (1, 3)])
    steps_w = plane_gather_steps(w_src, w_all, send_sems, recv_sems, 0)
    steps_r = line_gather_steps(route_src, route_all, send_sems, recv_sems, N_PLANE)
    steps_t = line_gather_steps(tok_src, tok_all, send_sems, recv_sems, N_PLANE + N_AG)
    next(steps_w)
    next(steps_r)
    next(steps_t)
    for steps in (steps_r, steps_w, steps_t):
        next(steps)
    next(steps_w)
    for steps in (steps_r, steps_t):
        for _ in steps:
            pass
    n_layers, _, _, n_mine, n_tok = route.shape
    n_half = n_chip // 2
    loc = lax.broadcasted_iota(jnp.int32, (n_mine, n_tok), 0)
    mine = ((z * 16 + loc // n_half) * n_chip + dp * n_half + lax.rem(loc, n_half)).astype(F32)
    row = lax.broadcasted_iota(jnp.int32, (n_tok, n_tok), 0)
    col = lax.broadcasted_iota(jnp.int32, (n_tok, n_tok), 1)
    before = jnp.where(row < col, 1.0, 0.0).astype(BF16)
    top_k = route_src.shape[0] // (4 * n_layers)
    for layer in range(n_layers):
        for s in range(8):
            rows = route_all[s, layer * 4 * top_k:(layer + 1) * 4 * top_k, :].astype(F32)
            used = jnp.zeros((n_mine, n_tok), F32)
            gates = [jnp.zeros((n_mine, n_tok), F32) for _ in range(3)]
            for j in range(top_k):
                hit = jnp.broadcast_to(rows[j:j + 1], mine.shape) == mine
                used = jnp.where(hit, 1.0, used)
                for k in range(3):
                    val = rows[(k + 1) * top_k + j:(k + 1) * top_k + j + 1]
                    gates[k] = jnp.where(hit, jnp.broadcast_to(val, mine.shape), gates[k])
            pos = nn(used.astype(BF16), before)
            route[layer, 0, s] = jnp.where(used > 0.5, pos, -1.0)
            for k in range(3):
                route[layer, 1 + k, s] = gates[k]
    for _ in steps_w:
        pass


def open_line(tok_src, route_src, w_src, n_layers, n_chip, collective_id):
    n_tok = route_src.shape[1]
    n_mine = 16 * n_chip // 2
    n_sem = N_PLANE + 2 * N_AG
    return pl.pallas_call(
        functools.partial(open_kernel, n_chip), name='open_line',
        out_shape=[jax.ShapeDtypeStruct((8,) + tok_src.shape, BF16),
                   jax.ShapeDtypeStruct((n_layers, 4, 8, n_mine, n_tok), F32),
                   jax.ShapeDtypeStruct((16,) + w_src.shape, BF16)],
        in_specs=[VMEM] * 3, out_specs=[VMEM] * 3,
        scratch_shapes=[pltpu.VMEM((8,) + route_src.shape, BF16),
                        pltpu.SemaphoreType.DMA((n_sem,)), pltpu.SemaphoreType.DMA((n_sem,))],
        compiler_params=params(collective_id))(tok_src, route_src, w_src)


def silu_parts(pre_gate):
    sig_val = jax.nn.sigmoid(pre_gate)
    return pre_gate * sig_val, sig_val * (1.0 + pre_gate * (1.0 - sig_val))


def split3(val):
    hi = lax.reduce_precision(val, 8, 7)
    rest = val - hi
    mid = lax.reduce_precision(rest, 8, 7)
    return hi, mid, rest - mid


def dot(spec, a, b):
    return jnp.einsum(spec, a, b, preferred_element_type=F32)


CHUNK = 8
SLOT = 32


def pick(pos_row, slots):
    return jnp.broadcast_to(pos_row, slots.shape) == slots


def one_hot(pos, source, values=None):
    n_tok = pos.shape[2]
    slots = lax.broadcasted_iota(jnp.int32, (SLOT, n_tok), 0).astype(F32)
    blocks = []
    for e in range(CHUNK):
        mask = pick(pos[source, e:e + 1, :], slots)
        val = 1.0 if values is None else jnp.broadcast_to(values[e:e + 1], mask.shape)
        blocks.append(jnp.where(mask, val, 0.0))
    return jnp.concatenate(blocks, axis=0)


def nn(a, b):
    return lax.dot_general(a, b, (((1,), (0,)), ((), ())), preferred_element_type=F32)


def nt(a, b):
    return lax.dot_general(a, b, (((1,), (1,)), ((), ())), preferred_element_type=F32)


def tn(a, b):
    return lax.dot_general(a, b, (((0,), (0,)), ((), ())), preferred_element_type=F32)


def forward_kernel(pos, u_all, w_in, recv, pre_gate, pre_up, hidden):
    for s in range(8):
        rows = nn(one_hot(pos, s).astype(BF16), u_all[s]).astype(BF16)
        for e in range(CHUNK):
            recv[e, s * SLOT:(s + 1) * SLOT, :] = rows[e * SLOT:(e + 1) * SLOT]
    for e in range(CHUNK):
        w_both = jnp.concatenate([w_in[e // 2, 0, e % 2], w_in[e // 2, 1, e % 2]], axis=1)
        both = nn(recv[e], w_both)
        a, b = both[:, :128], both[:, 128:]
        act, _ = silu_parts(a)
        pre_gate[e] = a
        pre_up[e] = b
        hidden[e] = (act * b).astype(BF16)


def route_specs(route, layer, kinds):
    return [pl.BlockSpec((None, None, 8, CHUNK, route.shape[4]), lambda i, k=k: (layer, k, 0, i, 0)) for k in kinds]


def token_spec(tok_all, n_tok, part):
    return pl.BlockSpec((8, n_tok, tok_all.shape[2]), lambda i: (0, part, 0))


def local_params():
    return pltpu.CompilerParams(vmem_limit_bytes=60 * 1024 * 1024)


def expert_forward(route, layer, u_all, weights):
    n_mine, n_tok = route.shape[3:]
    width = u_all.shape[2]
    ff = weights.shape[4]
    rows = 8 * SLOT
    per = lambda last: pl.BlockSpec((CHUNK, rows, last), lambda i: (i, 0, 0))
    return pl.pallas_call(
        forward_kernel, name='expert_forward', grid=(n_mine // CHUNK,),
        out_shape=[jax.ShapeDtypeStruct((n_mine, rows, width), BF16),
                   jax.ShapeDtypeStruct((n_mine, rows, ff), F32),
                   jax.ShapeDtypeStruct((n_mine, rows, ff), F32),
                   jax.ShapeDtypeStruct((n_mine, rows, ff), BF16)],
        in_specs=route_specs(route, layer, (0,)) + [
                  token_spec(u_all, n_tok, 0),
                  pl.BlockSpec((CHUNK // 2, 2, 2, width, ff), lambda i: (i, 0, 0, 0, 0))],
        out_specs=[per(width), per(ff), per(ff), per(ff)],
        compiler_params=local_params())(route, u_all, weights)


def combine_kernel(n_left, pos, hi, mid, lo, *refs):
    lefts, w_out, part, rows = refs[:n_left], refs[n_left], refs[n_left + 1], refs[n_left + 2]
    for e in range(CHUNK):
        left = jnp.concatenate([ref[e] for ref in lefts], axis=1)
        right = jnp.concatenate([w_out[e // 2, k, e % 2] for k in range(n_left)], axis=1)
        rows[e] = nt(left, right).astype(BF16)
    for s in range(8):
        mine = jnp.concatenate([rows[e, s * SLOT:(s + 1) * SLOT, :] for e in range(CHUNK)], axis=0)
        val = tn(one_hot(pos, s, lo[s]).astype(BF16), mine)
        val = val + tn(one_hot(pos, s, mid[s]).astype(BF16), mine)
        val = val + tn(one_hot(pos, s, hi[s]).astype(BF16), mine)

        @pl.when(pl.program_id(0) == 0)
        def _(val=val, s=s):
            part[s] = val

        @pl.when(pl.program_id(0) > 0)
        def _(val=val, s=s):
            part[s] = part[s] + val


def expert_combine(route, layer, lefts, weights, which):
    n_mine, n_tok = route.shape[3:]
    width, ff = weights.shape[3:]
    rows = 8 * SLOT
    n_left = len(lefts)
    per = pl.BlockSpec((CHUNK, rows, ff), lambda i: (i, 0, 0))
    return pl.pallas_call(
        functools.partial(combine_kernel, n_left), name='expert_combine', grid=(n_mine // CHUNK,),
        out_shape=jax.ShapeDtypeStruct((8, n_tok, width), F32),
        in_specs=route_specs(route, layer, (0, 1, 2, 3)) + [per] * n_left
        + [pl.BlockSpec((CHUNK // 2, n_left, 2, width, ff), lambda i: (i, which // n_left, 0, 0, 0))],
        out_specs=pl.BlockSpec((8, n_tok, width), lambda i: (0, 0, 0)),
        scratch_shapes=[pltpu.VMEM((CHUNK, rows, width), BF16)],
        compiler_params=local_params())(*[route] * 4, *lefts, weights)


def backward_kernel(pos, hi, mid, lo, dy_all, w_out, recv, pre_gate, pre_up, hidden, pack, d_gate, d_up, grad_in):
    for s in range(8):
        sel = one_hot(pos, s).astype(BF16)
        gate_slot = jnp.sum(one_hot(pos, s, (hi[s] + mid[s]) + lo[s]), axis=1, keepdims=True)
        rows = (gate_slot * nn(sel, dy_all[s])).astype(BF16)
        for e in range(CHUNK):
            grad_in[e, s * SLOT:(s + 1) * SLOT, :] = rows[e * SLOT:(e + 1) * SLOT]
    for e in range(CHUNK):
        c = grad_in[e]
        d_hidden = nn(c, w_out[e // 2, 0, e % 2])
        act, slope = silu_parts(pre_gate[e])
        da = (d_hidden * pre_up[e] * slope).astype(BF16)
        db = (d_hidden * act).astype(BF16)
        d_gate[e] = da
        d_up[e] = db
        both = tn(recv[e], jnp.concatenate([da, db], axis=1)).astype(BF16)
        pack[e // 2, 0, e % 2] = both[:, :128]
        pack[e // 2, 1, e % 2] = both[:, 128:]
        pack[e // 2, 2, e % 2] = tn(c, hidden[e]).astype(BF16)


def expert_backward(route, layer, dy_all, part, weights, recv, pre_gate, pre_up, hidden):
    n_mine, n_tok = route.shape[3:]
    width, ff = weights.shape[3:]
    rows = 8 * SLOT
    per = lambda last: pl.BlockSpec((CHUNK, rows, last), lambda i: (i, 0, 0))
    return pl.pallas_call(
        backward_kernel, name='expert_backward', grid=(n_mine // CHUNK,),
        out_shape=[jax.ShapeDtypeStruct(weights.shape, BF16),
                   jax.ShapeDtypeStruct((n_mine, rows, ff), BF16),
                   jax.ShapeDtypeStruct((n_mine, rows, ff), BF16)],
        in_specs=route_specs(route, layer, (0, 1, 2, 3)) + [
                  token_spec(dy_all, n_tok, part),
                  pl.BlockSpec((CHUNK // 2, 1, 2, width, ff), lambda i: (i, 2, 0, 0, 0)),
                  per(width), per(ff), per(ff), per(ff)],
        out_specs=[pl.BlockSpec((CHUNK // 2, 3, 2, width, ff), lambda i: (i, 0, 0, 0, 0)), per(ff), per(ff)],
        scratch_shapes=[pltpu.VMEM((CHUNK, rows, width), BF16)],
        compiler_params=local_params())(*[route] * 4, dy_all, weights, recv, pre_gate, pre_up, hidden)


def solution(mesh):
    m4 = Mesh(mesh.devices.reshape(4, 4, 4, 2), ('z', 'y', 'x', 'dp'))
    ep = ('z', 'y', 'x')
    tok_spec = P(('dp',) + ep, None)
    route_spec = P(None, ('dp',) + ep, None)
    whole_spec = P(None, None, None)
    expert_spec = P(None, ep, None, None)

    def device_body(tokens, d_out, expert_ids, gate_vals, w_mix, w_gate, w_up, w_down):
        n_layers = w_mix.shape[0]
        n_chip = w_gate.shape[1]
        n_half = n_chip // 2
        _, d_model = tokens.shape
        ff = w_gate.shape[3]
        dp = lax.axis_index('dp')

        def own_weights(layer):
            wg = lax.dynamic_slice_in_dim(w_gate[layer], dp * n_half, n_half, 0)
            wu = lax.dynamic_slice_in_dim(w_up[layer], dp * n_half, n_half, 0)
            wd = lax.dynamic_slice_in_dim(w_down[layer], dp * n_half, n_half, 0)
            return jnp.stack([wg, wu, jnp.swapaxes(wd, 1, 2)], axis=0)

        def scatter_grads(pack):
            part = lax.psum_scatter(pack.reshape(16 * 3 * n_half * d_model, ff), ('y', 'x'),
                                    scatter_dimension=0, tiled=True)
            return part

        def finish_grads(part):
            other = lax.ppermute(part, 'dp', [(0, 1), (1, 0)])
            lo = jnp.where(dp == 0, part, other).reshape(3, n_half, d_model, ff)
            hi = jnp.where(dp == 0, other, part).reshape(3, n_half, d_model, ff)
            both = jnp.concatenate([lo, hi], axis=1)
            return both[0], both[1], jnp.swapaxes(both[2], 1, 2)

        route_src = []
        for layer in range(n_layers):
            route_src.append(expert_ids[layer].astype(BF16))
            route_src.extend(part.astype(BF16) for part in split3(gate_vals[layer]))
        route_src = jnp.concatenate(route_src, axis=1).T

        u_act = (tokens.astype(F32) + dot('td,de->te', tokens, w_mix[0])).astype(BF16)
        first = jnp.concatenate([u_act, d_out], axis=0)
        tok_all, route, w_first = open_line(first, route_src, own_weights(0), n_layers, n_chip, 1)
        own_top, w_first = lax.optimization_barrier((own_weights(1), w_first))
        w_top = lax.all_gather(own_top.reshape(3 * n_half * d_model, ff), ('y', 'x'), axis=0, tiled=False)
        w_top = w_top.reshape(16, 3, n_half, d_model, ff)

        low = expert_forward(route, 0, tok_all, w_first)
        part = expert_combine(route, 0, low[3:], w_first, 2)
        y_low, u_top, u_all = pass_line(part, u_act, w_mix[1], False, True, 2)

        w_top, u_all = lax.optimization_barrier((w_top, u_all))
        top = expert_forward(route, 1, u_all, w_top)
        pack, d_gate, d_up = expert_backward(route, 1, tok_all, 1, w_top, *top)
        grad_top = scatter_grads(pack)
        part = expert_combine(route, 1, (d_gate, d_up), w_top, 0)
        d_u, d_y, dy_all = pass_line(part, d_out, w_mix[1], True, True, 3)
        mix_top = dot('td,te->de', y_low, d_u).astype(BF16)

        pack, d_gate, d_up = expert_backward(route, 0, dy_all, 0, w_first, *low)
        grad_low = scatter_grads(pack)
        part_v = expert_combine(route, 0, (d_gate, d_up), w_first, 0)
        hidden, part_v = lax.optimization_barrier((top[3], part_v))
        part_y = expert_combine(route, 1, (hidden,), w_top, 2)
        d_tokens, layer_out, mix_out = close_line(part_v, d_y, w_mix[0], tokens, mix_top, part_y, u_top, 4)
        grad_top, d_tokens = lax.optimization_barrier((grad_top, d_tokens))
        grads = [finish_grads(grad_low), finish_grads(grad_top)]
        return (layer_out, d_tokens, mix_out) + tuple(jnp.stack([g[k] for g in grads]) for k in range(3))

    return jax.shard_map(device_body, mesh=m4,
                         in_specs=(tok_spec, tok_spec, route_spec, route_spec, whole_spec,
                                   expert_spec, expert_spec, expert_spec),
                         out_specs=(tok_spec, tok_spec, whole_spec, expert_spec, expert_spec, expert_spec),
                         check_vma=False)
```

time: 541 us -> 501 us (0.926)
  waiting for transfers between devices: 137 us -> 96.2 us
  Pallas kernels: 354 us -> 367 us
  other arithmetic: 18.2 us -> 6.21 us
    all_gather x2 -> x1, waiting for transfers between devices: 47.3 us -> 6.61 us  [device_body(): lax.all_gather(own_top.reshape(3 * n_half * d_model, ff), ('y', 'x'), axi...]
    pallas_call x3 -> x2, Pallas kernels: 101 us -> 141 us  [the longest x1 71 us: open_line(): pl.pallas_call(functools.partial(open_kernel, n_chip), name='open_line',...]
    pallas_call x3 -> x2, Pallas kernels: 110 us -> 83.8 us  [pass_line(): pl.pallas_call(functools.partial(pass_kernel, transpose, want_all), name=...]
  transfers between devices with their start and end apart: 6 -> 5, of which waited for: 3 -> 3; matrix products, arithmetic and copies ran while one was open for 5% -> 1% of each run, Pallas kernels for 45% -> 37%
where the time goes in v1:
time: 501 us
  Pallas kernels  367 us (73%)
  waiting for transfers between devices  96.2 us (19%)
  between operations  14 us (3%)
  local copies, waits for them, and re-layouts  13.5 us (3%)
  other arithmetic  6.21 us (1%)
    reduce_scatter x2, waiting for transfers between devices, scatter_grads(): lax.psum_scatter(pack.reshape(16 * 3 * n_half * d_model, ff), ('y', 'x'),...  88.7 us
    pallas_call x2, Pallas kernels, pass_line(): pl.pallas_call(functools.partial(pass_kernel, transpose, want_all), name=...  83.8 us
    pallas_call x4, Pallas kernels, expert_combine(): pl.pallas_call(functools.partial(combine_kernel, n_left), name='expert_co...  82.6 us
    pallas_call x1, Pallas kernels, open_line(): pl.pallas_call(functools.partial(open_kernel, n_chip), name='open_line',...  71 us
    pallas_call x1, Pallas kernels, close_line(): pl.pallas_call(close_kernel, name='close_line', out_shape=[block, block,...  69.9 us
    pallas_call x2, Pallas kernels, expert_backward(): pl.pallas_call(backward_kernel, name='expert_backward', grid=(n_mine // C...  37.6 us
    pallas_call x2, Pallas kernels, expert_forward(): pl.pallas_call(forward_kernel, name='expert_forward', grid=(n_mine // CHU...  22.4 us
  transfers between devices with their start and end apart: 5, of which 3 were waited for; matrix products, arithmetic and copies ran while one was open for 1% of the time, Pallas kernels for 37%

profile of v1, /device:TPU:1, one launch (start us, length us, event | category | flops | bytes accessed | tf_op | source)
XLA Modules:
  0.0 500.8 jit_solution(11370855302628345316)
XLA Ops:
  7.2 2.3 fusion.11
  10.6 1.1 copy.30.base
  11.8 1.1 dynamic-slice_bitcast_fusion
  16.1 71.0 %open_line.1 = (bf16[8,512,448]{2,1,0:T(8,128)(2,1)}, f32[2,4,8,32,256]{4,3,2,1,0:T(8,128)}, bf16[16,3,2,448,128]{4,3,2,1,0:T(8,128)(2,1)}) custom-call(bf16[512,448]{1,0:T(8,128)(2,1)} %pad_maximum_fusion.5.tok_src, bf16[64,256]{1,0:T(8,128)(2,1)} %bitcast.86, bf16[3,2,448,128]{3,2,1,0:T(8,128)(2,1)} %pad_maximum_fusion.3.w_src), custom_call_target="tpu_custom_call" | custom-call | tf_op jit(solution)/shard_map/open_line/pallas_call | solution.py:374
  88.2 11.2 %expert_forward.2 = (bf16[32,256,448]{2,1,0:T(8,128)(2,1)}, f32[32,256,128]{2,1,0:T(8,128)}, f32[32,256,128]{2,1,0:T(8,128)}, bf16[32,256,128]{2,1,0:T(8,128)(2,1)}) custom-call(f32[2,4,8,32,256]{4,3,2,1,0:T(8,128)} %get-tuple-element.40.pos.hi.mid.lo, bf16[8,512,448]{2,1,0:T(8,128)(2,1)} %get-tuple-element.43.u_all.dy_all, ...), custom_call_target="tpu_custom_call" | custom-call | tf_op jit(solution)/shard_map/expert_forward/pallas_call | solution.py:465
  99.5 20.3 %expert_combine.4.part = f32[8,256,448]{2,1,0:T(8,128)} custom-call(f32[2,4,8,32,256]{4,3,2,1,0:T(8,128)} %get-tuple-element.40.pos.hi.mid.lo, f32[2,4,8,32,256]{4,3,2,1,0:T(8,128)} %get-tuple-element.40.pos.hi.mid.lo, f32[2,4,8,32,256]{4,3,2,1,0:T(8,128)} %get-tuple-element.40.pos.hi.mid.lo, f32[2,4,8,32,256]{4,3,2,1,0:T(8,128)} %get-tuple-element.40.pos.hi.mid.lo, ...), custom_call_target="tpu_custom_call" | custom-call | tf_op jit(solution)/shard_map/expert_combine/pallas_call | solution.py:505
  120.8 42.5 %pass_line.2 = (bf16[256,448]{1,0:T(8,128)(2,1)}, bf16[256,448]{1,0:T(8,128)(2,1)}, bf16[8,256,448]{2,1,0:T(8,128)(2,1)}) custom-call(f32[8,256,448]{2,1,0:T(8,128)} %expert_combine.4.part, bf16[256,448]{1,0:T(8,128)(2,1)} %copy-done.1, bf16[448,448]{1,0:T(8,128)(2,1)} %get-tuple-element.103.w_mix), custom_call_target="tpu_custom_call" | custom-call | tf_op jit(solution)/shard_map/pass_line/pallas_call | solution.py:151
  163.3 6.6 %all-gather.2.cloned.1.call-done = bf16[16,2688,128]{2,1,0:T(8,128)(2,1)} async-done(((bf16[1,2688,128]{2,1,0:T(8,128)(2,1)}), bf16[16,2688,128]{2,1,0:T(8,128)(2,1)}) %all-gather.2.cloned.1.call-update) | async-done | bytes 11010064 | tf_op jit(solution)/shard_map/all_gather | solution.py:599
  169.9 11.2 %expert_forward.3 = (bf16[32,256,448]{2,1,0:T(8,128)(2,1)}, f32[32,256,128]{2,1,0:T(8,128)}, f32[32,256,128]{2,1,0:T(8,128)}, bf16[32,256,128]{2,1,0:T(8,128)(2,1)}) custom-call(f32[2,4,8,32,256]{4,3,2,1,0:T(8,128)} %get-tuple-element.40.pos.hi.mid.lo, bf16[8,256,448]{2,1,0:T(8,128)(2,1)} %get-tuple-element.47.u_all, bf16[16,3,2,448,128]{4,3,2,1,0:T(8,128)(2,1)} %bitcast.75), custom_call_target="tpu_custom_call" | custom-call | tf_op jit(solution)/shard_map/expert_forward/pallas_call | solution.py:465
  181.1 18.8 %expert_backward.2 = (bf16[16,3,2,448,128]{4,3,2,1,0:T(8,128)(2,1)}, bf16[32,256,128]{2,1,0:T(8,128)(2,1)}, bf16[32,256,128]{2,1,0:T(8,128)(2,1)}) custom-call(f32[2,4,8,32,256]{4,3,2,1,0:T(8,128)} %get-tuple-element.40.pos.hi.mid.lo, f32[2,4,8,32,256]{4,3,2,1,0:T(8,128)} %get-tuple-element.40.pos.hi.mid.lo, ...), custom_call_target="tpu_custom_call" | custom-call | tf_op jit(solution)/shard_map/expert_backward/pallas_call | solution.py:541
  199.9 21.2 %expert_combine.5.part = f32[8,256,448]{2,1,0:T(8,128)} custom-call(f32[2,4,8,32,256]{4,3,2,1,0:T(8,128)} %get-tuple-element.40.pos.hi.mid.lo, f32[2,4,8,32,256]{4,3,2,1,0:T(8,128)} %get-tuple-element.40.pos.hi.mid.lo, f32[2,4,8,32,256]{4,3,2,1,0:T(8,128)} %get-tuple-element.40.pos.hi.mid.lo, f32[2,4,8,32,256]{4,3,2,1,0:T(8,128)} %get-tuple-element.40.pos.hi.mid.lo, ...), custom_call_target="tpu_custom_call" | custom-call | tf_op jit(solution)/shard_map/expert_combine/pallas_call | solution.py:505
  221.1 41.4 %pass_line.3 = (bf16[256,448]{1,0:T(8,128)(2,1)}, bf16[256,448]{1,0:T(8,128)(2,1)}, bf16[8,256,448]{2,1,0:T(8,128)(2,1)}) custom-call(f32[8,256,448]{2,1,0:T(8,128)} %expert_combine.5.part, bf16[256,448]{1,0:T(8,128)(2,1)} %copy-done, bf16[448,448]{1,0:T(8,128)(2,1)} %get-tuple-element.103.w_mix), custom_call_target="tpu_custom_call" | custom-call | tf_op jit(solution)/shard_map/pass_line/pallas_call | solution.py:151
  262.5 18.8 %expert_backward.3 = (bf16[16,3,2,448,128]{4,3,2,1,0:T(8,128)(2,1)}, bf16[32,256,128]{2,1,0:T(8,128)(2,1)}, bf16[32,256,128]{2,1,0:T(8,128)(2,1)}) custom-call(f32[2,4,8,32,256]{4,3,2,1,0:T(8,128)} %get-tuple-element.40.pos.hi.mid.lo, f32[2,4,8,32,256]{4,3,2,1,0:T(8,128)} %get-tuple-element.40.pos.hi.mid.lo, ...), custom_call_target="tpu_custom_call" | custom-call | tf_op jit(solution)/shard_map/expert_backward/pallas_call | solution.py:541
  282.0 88.7 %reduce-scatter.5.cloned.1.call-done = bf16[2688,128]{1,0:T(8,128)(2,1)} async-done(((bf16[43008,128]{1,0:T(8,128)(2,1)}), bf16[2688,128]{1,0:T(8,128)(2,1)}) %reduce-scatter.5.cloned.1.call-update) | async-done | bytes 688144 | tf_op jit(solution)/shard_map/reduce_scatter | solution.py:578
  370.7 1.7 collective-permute-start
  373.3 20.8 %expert_combine.6.part_v = f32[8,256,448]{2,1,0:T(8,128)} custom-call(f32[2,4,8,32,256]{4,3,2,1,0:T(8,128)} %get-tuple-element.40.pos.hi.mid.lo, f32[2,4,8,32,256]{4,3,2,1,0:T(8,128)} %get-tuple-element.40.pos.hi.mid.lo, f32[2,4,8,32,256]{4,3,2,1,0:T(8,128)} %get-tuple-element.40.pos.hi.mid.lo, f32[2,4,8,32,256]{4,3,2,1,0:T(8,128)} %get-tuple-element.40.pos.hi.mid.lo, ...), custom_call_target="tpu_custom_call" | custom-call | tf_op jit(solution)/shard_map/expert_combine/pallas_call | solution.py:505
  394.0 20.3 %expert_combine.7.part_y = f32[8,256,448]{2,1,0:T(8,128)} custom-call(f32[2,4,8,32,256]{4,3,2,1,0:T(8,128)} %get-tuple-element.40.pos.hi.mid.lo, f32[2,4,8,32,256]{4,3,2,1,0:T(8,128)} %get-tuple-element.40.pos.hi.mid.lo, f32[2,4,8,32,256]{4,3,2,1,0:T(8,128)} %get-tuple-element.40.pos.hi.mid.lo, f32[2,4,8,32,256]{4,3,2,1,0:T(8,128)} %get-tuple-element.40.pos.hi.mid.lo, ...), custom_call_target="tpu_custom_call" | custom-call | tf_op jit(solution)/shard_map/expert_combine/pallas_call | solution.py:505
  414.3 1.1 convolution_convert_fusion.mix_top
  415.4 69.9 %close_line.1 = (bf16[256,448]{1,0:T(8,128)(2,1)}, bf16[256,448]{1,0:T(8,128)(2,1)}, bf16[2,448,448]{2,1,0:T(8,128)(2,1)}) custom-call(f32[8,256,448]{2,1,0:T(8,128)} %expert_combine.6.part_v, bf16[256,448]{1,0:T(8,128)(2,1)} %get-tuple-element.62.base_v, bf16[448,448]{1,0:T(8,128)(2,1)} %get-tuple-element.102.w_mix, bf16[256,448]{1,0:T(8,128)(2,1)} %copy.32.x_in, ...), custom_call_target="tpu_custom_call" | custom-call | tf_op jit(solution)/shard_map/close_line/pallas_call | solution.py:248
  485.3 1.8 copy.33
  487.2 1.8 copy.34
  490.3 1.0 pad_maximum_fusion.2
  491.3 1.0 pad_maximum_fusion.1
  492.3 1.0 pad_maximum_fusion
  (63 shorter events, 10.3 us)
Async XLA Ops:
  7.2 2.3 copy-start.4
  7.2 2.4 copy-start.5
  7.2 162.7 %all-gather.2.cloned.1.call-start = ((), (), s32[]{:S(2)}) async-start(), calls=%async_computation.2 | async-start | bytes 11698176 | tf_op jit(solution)/shard_map/all_gather | solution.py:599
  9.5 0.9 copy-start.3
  9.5 2.2 copy-start.13
  9.5 2.2 copy-start.11
  9.6 4.3 copy-start.2
  11.7 3.4 copy-start
  11.8 3.3 copy-start.12
  14.2 72.8 %copy-start.1 = (bf16[256,448]{1,0:T(8,128)(2,1)}, bf16[256,448]{1,0:T(8,128)(2,1)S(1)}, u32[]{:S(2)}) copy-start(bf16[256,448]{1,0:T(8,128)(2,1)S(1)} %fusion.base) | copy-start | bytes 688132
  88.0 282.7 %reduce-scatter.5.cloned.1.call-start = ((), (), s32[]{:S(2)}) async-start(), calls=%async_computation.4 | async-start | bytes 11698176 | tf_op jit(solution)/shard_map/reduce_scatter | solution.py:578
  281.3 205.8 %reduce-scatter.3.cloned.1.call-start = ((), (), s32[]{:S(2)}) async-start(), calls=%async_computation.3 | async-start | bytes 11698176 | tf_op jit(solution)/shard_map/reduce_scatter | solution.py:578
  370.7 118.3 %collective-permute-start = (bf16[2688,128]{1,0:T(8,128)(2,1)}, bf16[2688,128]{1,0:T(8,128)(2,1)S(1)}, u32[]{:S(2)}, u32[]{:S(2)}) collective-permute-start(bf16[2688,128]{1,0:T(8,128)(2,1)} %reduce-scatter.5.cloned.1.call-done), channel_id=1, source_target_pairs={{0,1},{1,0},{2,3},{3,2},{4,5},{5,4},{6,7},{7,6},{8,9},{9,8},{10,11... | collective-permute-start | bytes 2064392 | tf_op jit(solution)/shard_map/ppermute | solution.py:583
  394.0 20.3 %copy-start.9 = (bf16[256,448]{1,0:T(8,128)(2,1)S(1)}, bf16[256,448]{1,0:T(8,128)(2,1)}, u32[]{:S(2)}) copy-start(bf16[256,448]{1,0:T(8,128)(2,1)} %get-tuple-element.63) | copy-start | bytes 688132
  394.0 20.3 %copy-start.10 = (bf16[256,448]{1,0:T(8,128)(2,1)S(1)}, bf16[256,448]{1,0:T(8,128)(2,1)}, u32[]{:S(2)}) copy-start(bf16[256,448]{1,0:T(8,128)(2,1)} %get-tuple-element.64) | copy-start | bytes 688132
  415.4 73.6 %copy-start.8 = (bf16[2688,128]{1,0:T(8,128)(2,1)S(1)}, bf16[2688,128]{1,0:T(8,128)(2,1)}, u32[]{:S(2)}) copy-start(bf16[2688,128]{1,0:T(8,128)(2,1)} %reduce-scatter.5.cloned.1.call-done) | copy-start | bytes 2064388
  487.1 2.4 collective-permute-start.1
  489.0 1.1 copy-start.7
  491.3 2.0 copy-start.6
Sparse Core Ops, SparseCore 0:
  88.1 81.6 all-gather.1
  281.4 89.2 reduce-scatter.4
  374.2 96.2 reduce-scatter.2

commit v2 on v1

--- a/solution.py
+++ b/solution.py
@@ -399,20 +399,17 @@
 
 
 CHUNK = 8
-SLOT = 32
-
-
-def pick(pos_row, slots):
-    return jnp.broadcast_to(pos_row, slots.shape) == slots
+SLOT = 24
+ROWS = 8 * SLOT
 
 
 def one_hot(pos, source, values=None):
-    n_tok = pos.shape[2]
+    n_experts, n_tok = pos.shape[1:]
     slots = lax.broadcasted_iota(jnp.int32, (SLOT, n_tok), 0).astype(F32)
     blocks = []
-    for e in range(CHUNK):
-        mask = pick(pos[source, e:e + 1, :], slots)
-        val = 1.0 if values is None else jnp.broadcast_to(values[e:e + 1], mask.shape)
+    for e in range(n_experts):
+        mask = jnp.broadcast_to(pos[source, e:e + 1, :], slots.shape) == slots
+        val = 1.0 if values is None else jnp.broadcast_to(values[e:e + 1], slots.shape)
         blocks.append(jnp.where(mask, val, 0.0))
     return jnp.concatenate(blocks, axis=0)
 
@@ -429,127 +426,174 @@
     return lax.dot_general(a, b, (((0,), (0,)), ((), ())), preferred_element_type=F32)
 
 
+def select_rows(rows_of, out):
+    for pair in range(4):
+        both = [rows_of(2 * pair), rows_of(2 * pair + 1)]
+        for e in range(CHUNK):
+            val = jnp.concatenate([rows[e * SLOT:(e + 1) * SLOT] for rows in both], axis=0)
+            out[e, pair * 2 * SLOT:(pair + 1) * 2 * SLOT, :] = val.astype(BF16)
+
+
+def select_tokens(pos, u_all, recv):
+    select_rows(lambda s: nn(one_hot(pos, s).astype(BF16), u_all[s]), recv)
+
+
+def select_grads(pos, hi, mid, lo, dy_all, grad_in):
+    def rows_of(s):
+        gate_slot = jnp.sum(one_hot(pos, s, (hi[s] + mid[s]) + lo[s]), axis=1, keepdims=True)
+        return gate_slot * nn(one_hot(pos, s).astype(BF16), dy_all[s])
+
+    select_rows(rows_of, grad_in)
+
+
+def hidden_of(rows, w_in, e):
+    both = nn(rows, jnp.concatenate([w_in[e // 2, 0, e % 2], w_in[e // 2, 1, e % 2]], axis=1))
+    ff = both.shape[1] // 2
+    a, b = both[:, :ff], both[:, ff:]
+    act, _ = silu_parts(a)
+    return a, b, (act * b).astype(BF16)
+
+
+def expert_grads(c, rows, a, b, h, w_down, e, pack, d_gate, d_up):
+    d_hidden = nn(c, w_down)
+    act, slope = silu_parts(a)
+    da = (d_hidden * b * slope).astype(BF16)
+    db = (d_hidden * act).astype(BF16)
+    d_gate[e] = da
+    d_up[e] = db
+    both = tn(rows, jnp.concatenate([da, db], axis=1)).astype(BF16)
+    ff = both.shape[1] // 2
+    pack[e // 2, 0, e % 2] = both[:, :ff]
+    pack[e // 2, 1, e % 2] = both[:, ff:]
+    pack[e // 2, 2, e % 2] = tn(c, h).astype(BF16)
+
+
 def forward_kernel(pos, u_all, w_in, recv, pre_gate, pre_up, hidden):
-    for s in range(8):
-        rows = nn(one_hot(pos, s).astype(BF16), u_all[s]).astype(BF16)
-        for e in range(CHUNK):
-            recv[e, s * SLOT:(s + 1) * SLOT, :] = rows[e * SLOT:(e + 1) * SLOT]
+    select_tokens(pos, u_all, recv)
     for e in range(CHUNK):
-        w_both = jnp.concatenate([w_in[e // 2, 0, e % 2], w_in[e // 2, 1, e % 2]], axis=1)
-        both = nn(recv[e], w_both)
-        a, b = both[:, :128], both[:, 128:]
-        act, _ = silu_parts(a)
-        pre_gate[e] = a
-        pre_up[e] = b
-        hidden[e] = (act * b).astype(BF16)
-
-
-def route_specs(route, layer, kinds):
-    return [pl.BlockSpec((None, None, 8, CHUNK, route.shape[4]), lambda i, k=k: (layer, k, 0, i, 0)) for k in kinds]
-
-
-def token_spec(tok_all, n_tok, part):
-    return pl.BlockSpec((8, n_tok, tok_all.shape[2]), lambda i: (0, part, 0))
-
-
-def local_params():
-    return pltpu.CompilerParams(vmem_limit_bytes=60 * 1024 * 1024)
-
-
-def expert_forward(route, layer, u_all, weights):
-    n_mine, n_tok = route.shape[3:]
-    width = u_all.shape[2]
-    ff = weights.shape[4]
-    rows = 8 * SLOT
-    per = lambda last: pl.BlockSpec((CHUNK, rows, last), lambda i: (i, 0, 0))
-    return pl.pallas_call(
-        forward_kernel, name='expert_forward', grid=(n_mine // CHUNK,),
-        out_shape=[jax.ShapeDtypeStruct((n_mine, rows, width), BF16),
-                   jax.ShapeDtypeStruct((n_mine, rows, ff), F32),
-                   jax.ShapeDtypeStruct((n_mine, rows, ff), F32),
-                   jax.ShapeDtypeStruct((n_mine, rows, ff), BF16)],
-        in_specs=route_specs(route, layer, (0,)) + [
-                  token_spec(u_all, n_tok, 0),
-                  pl.BlockSpec((CHUNK // 2, 2, 2, width, ff), lambda i: (i, 0, 0, 0, 0))],
-        out_specs=[per(width), per(ff), per(ff), per(ff)],
-        compiler_params=local_params())(route, u_all, weights)
+        pre_gate[e], pre_up[e], hidden[e] = hidden_of(recv[e], w_in, e)
+
+
+def backward_kernel(pos, hi, mid, lo, dy_all, w_out, recv, pre_gate, pre_up, hidden, pack, d_gate, d_up, grad_in):
+    select_grads(pos, hi, mid, lo, dy_all, grad_in)
+    for e in range(CHUNK):
+        expert_grads(grad_in[e], recv[e], pre_gate[e], pre_up[e], hidden[e], w_out[e // 2, 0, e % 2], e,
+                     pack, d_gate, d_up)
+
+
+def select_kernel(pos, hi, mid, lo, u_all, dy_all, recv, grad_in):
+    select_tokens(pos, u_all, recv)
+    select_grads(pos, hi, mid, lo, dy_all, grad_in)
+
+
+def top_kernel(recv, grad_in, w_all, pack, d_gate, d_up, hidden):
+    for e in range(CHUNK):
+        rows = recv[e]
+        a, b, h = hidden_of(rows, w_all, e)
+        hidden[e] = h
+        expert_grads(grad_in[e], rows, a, b, h, w_all[e // 2, 2, e % 2], e, pack, d_gate, d_up)
 
 
 def combine_kernel(n_left, pos, hi, mid, lo, *refs):
     lefts, w_out, part, rows = refs[:n_left], refs[n_left], refs[n_left + 1], refs[n_left + 2]
+    step = pl.program_id(0)
     for e in range(CHUNK):
         left = jnp.concatenate([ref[e] for ref in lefts], axis=1)
         right = jnp.concatenate([w_out[e // 2, k, e % 2] for k in range(n_left)], axis=1)
-        rows[e] = nt(left, right).astype(BF16)
-    for s in range(8):
-        mine = jnp.concatenate([rows[e, s * SLOT:(s + 1) * SLOT, :] for e in range(CHUNK)], axis=0)
-        val = tn(one_hot(pos, s, lo[s]).astype(BF16), mine)
-        val = val + tn(one_hot(pos, s, mid[s]).astype(BF16), mine)
-        val = val + tn(one_hot(pos, s, hi[s]).astype(BF16), mine)
-
-        @pl.when(pl.program_id(0) == 0)
-        def _(val=val, s=s):
-            part[s] = val
-
-        @pl.when(pl.program_id(0) > 0)
-        def _(val=val, s=s):
-            part[s] = part[s] + val
+        rows[step * CHUNK + e] = nt(left, right).astype(BF16).astype(F32)
+
+    @pl.when(step == pl.num_programs(0) - 1)
+    def _():
+        def source(s, carry):
+            slots = pl.ds(pl.multiple_of(s * SLOT, 8), SLOT)
+            mine = jnp.concatenate([rows[e, slots, :] for e in range(rows.shape[0])], axis=0).astype(BF16)
+            val = tn(one_hot(pos, s, lo[s]).astype(BF16), mine)
+            val = val + tn(one_hot(pos, s, mid[s]).astype(BF16), mine)
+            part[s] = val + tn(one_hot(pos, s, hi[s]).astype(BF16), mine)
+            return carry
+
+        lax.fori_loop(0, 8, source, 0)
+
+
+def route_specs(route, layer, kinds, n_experts=CHUNK):
+    pick = (lambda i: i) if n_experts == CHUNK else (lambda i: 0)
+    return [pl.BlockSpec((None, None, 8, n_experts, route.shape[4]), lambda i, k=k: (layer, k, 0, pick(i), 0))
+            for k in kinds]
+
+
+def token_spec(tok_all, n_tok, part):
+    return pl.BlockSpec((8, n_tok, tok_all.shape[2]), lambda i: (0, part, 0))
+
+
+def per_expert(last):
+    return pl.BlockSpec((CHUNK, ROWS, last), lambda i: (i, 0, 0))
+
+
+def weight_spec(weights, kinds, first):
+    return pl.BlockSpec((CHUNK // 2, kinds, 2) + weights.shape[3:], lambda i: (i, first // kinds, 0, 0, 0))
+
+
+def local_call(kernel, n_mine, outs, in_specs, out_specs, scratch=()):
+    return pl.pallas_call(
+        kernel, grid=(n_mine // CHUNK,), out_shape=outs, in_specs=in_specs, out_specs=out_specs,
+        scratch_shapes=list(scratch), compiler_params=pltpu.CompilerParams(vmem_limit_bytes=60 * 1024 * 1024))
+
+
+def per_slot(n_mine, last, dtype):
+    return jax.ShapeDtypeStruct((n_mine, ROWS, last), dtype)
+
+
+def expert_forward(route, layer, u_all, weights):
+    n_mine, n_tok = route.shape[3:]
+    width, ff = weights.shape[3:]
+    return local_call(
+        forward_kernel, n_mine,
+        [per_slot(n_mine, width, BF16), per_slot(n_mine, ff, F32), per_slot(n_mine, ff, F32), per_slot(n_mine, ff, BF16)],
+        route_specs(route, layer, (0,)) + [token_spec(u_all, n_tok, 0), weight_spec(weights, 2, 0)],
+        [per_expert(width), per_expert(ff), per_expert(ff), per_expert(ff)])(route, u_all, weights)
+
+
+def expert_backward(route, layer, dy_all, weights, recv, pre_gate, pre_up, hidden):
+    n_mine, n_tok = route.shape[3:]
+    width, ff = weights.shape[3:]
+    return local_call(
+        backward_kernel, n_mine,
+        [jax.ShapeDtypeStruct(weights.shape, BF16), per_slot(n_mine, ff, BF16), per_slot(n_mine, ff, BF16)],
+        route_specs(route, layer, (0, 1, 2, 3)) + [token_spec(dy_all, n_tok, 0), weight_spec(weights, 1, 2),
+                                                   per_expert(width), per_expert(ff), per_expert(ff), per_expert(ff)],
+        [weight_spec(weights, 3, 0), per_expert(ff), per_expert(ff)],
+        [pltpu.VMEM((CHUNK, ROWS, width), BF16)])(*[route] * 4, dy_all, weights, recv, pre_gate, pre_up, hidden)
+
+
+def expert_select(route, layer, u_all, dy_all, dy_part):
+    n_mine, n_tok = route.shape[3:]
+    width = u_all.shape[2]
+    return local_call(
+        select_kernel, n_mine, [per_slot(n_mine, width, BF16)] * 2,
+        route_specs(route, layer, (0, 1, 2, 3)) + [token_spec(u_all, n_tok, 0), token_spec(dy_all, n_tok, dy_part)],
+        [per_expert(width)] * 2)(*[route] * 4, u_all, dy_all)
+
+
+def expert_top(recv, grad_in, weights):
+    n_mine = recv.shape[0]
+    width, ff = weights.shape[3:]
+    return local_call(
+        top_kernel, n_mine,
+        [jax.ShapeDtypeStruct(weights.shape, BF16)] + [per_slot(n_mine, ff, BF16)] * 3,
+        [per_expert(width)] * 2 + [weight_spec(weights, 3, 0)],
+        [weight_spec(weights, 3, 0)] + [per_expert(ff)] * 3)(recv, grad_in, weights)
 
 
 def expert_combine(route, layer, lefts, weights, which):
     n_mine, n_tok = route.shape[3:]
     width, ff = weights.shape[3:]
-    rows = 8 * SLOT
-    n_left = len(lefts)
-    per = pl.BlockSpec((CHUNK, rows, ff), lambda i: (i, 0, 0))
-    return pl.pallas_call(
-        functools.partial(combine_kernel, n_left), name='expert_combine', grid=(n_mine // CHUNK,),
-        out_shape=jax.ShapeDtypeStruct((8, n_tok, width), F32),
-        in_specs=route_specs(route, layer, (0, 1, 2, 3)) + [per] * n_left
-        + [pl.BlockSpec((CHUNK // 2, n_left, 2, width, ff), lambda i: (i, which // n_left, 0, 0, 0))],
-        out_specs=pl.BlockSpec((8, n_tok, width), lambda i: (0, 0, 0)),
-        scratch_shapes=[pltpu.VMEM((CHUNK, rows, width), BF16)],
-        compiler_params=local_params())(*[route] * 4, *lefts, weights)
-
-
-def backward_kernel(pos, hi, mid, lo, dy_all, w_out, recv, pre_gate, pre_up, hidden, pack, d_gate, d_up, grad_in):
-    for s in range(8):
-        sel = one_hot(pos, s).astype(BF16)
-        gate_slot = jnp.sum(one_hot(pos, s, (hi[s] + mid[s]) + lo[s]), axis=1, keepdims=True)
-        rows = (gate_slot * nn(sel, dy_all[s])).astype(BF16)
-        for e in range(CHUNK):
-            grad_in[e, s * SLOT:(s + 1) * SLOT, :] = rows[e * SLOT:(e + 1) * SLOT]
-    for e in range(CHUNK):
-        c = grad_in[e]
-        d_hidden = nn(c, w_out[e // 2, 0, e % 2])
-        act, slope = silu_parts(pre_gate[e])
-        da = (d_hidden * pre_up[e] * slope).astype(BF16)
-        db = (d_hidden * act).astype(BF16)
-        d_gate[e] = da
-        d_up[e] = db
-        both = tn(recv[e], jnp.concatenate([da, db], axis=1)).astype(BF16)
-        pack[e // 2, 0, e % 2] = both[:, :128]
-        pack[e // 2, 1, e % 2] = both[:, 128:]
-        pack[e // 2, 2, e % 2] = tn(c, hidden[e]).astype(BF16)
-
-
-def expert_backward(route, layer, dy_all, part, weights, recv, pre_gate, pre_up, hidden):
-    n_mine, n_tok = route.shape[3:]
-    width, ff = weights.shape[3:]
-    rows = 8 * SLOT
-    per = lambda last: pl.BlockSpec((CHUNK, rows, last), lambda i: (i, 0, 0))
-    return pl.pallas_call(
-        backward_kernel, name='expert_backward', grid=(n_mine // CHUNK,),
-        out_shape=[jax.ShapeDtypeStruct(weights.shape, BF16),
-                   jax.ShapeDtypeStruct((n_mine, rows, ff), BF16),
-                   jax.ShapeDtypeStruct((n_mine, rows, ff), BF16)],
-        in_specs=route_specs(route, layer, (0, 1, 2, 3)) + [
-                  token_spec(dy_all, n_tok, part),
-                  pl.BlockSpec((CHUNK // 2, 1, 2, width, ff), lambda i: (i, 2, 0, 0, 0)),
-                  per(width), per(ff), per(ff), per(ff)],
-        out_specs=[pl.BlockSpec((CHUNK // 2, 3, 2, width, ff), lambda i: (i, 0, 0, 0, 0)), per(ff), per(ff)],
-        scratch_shapes=[pltpu.VMEM((CHUNK, rows, width), BF16)],
-        compiler_params=local_params())(*[route] * 4, dy_all, weights, recv, pre_gate, pre_up, hidden)
+    return local_call(
+        functools.partial(combine_kernel, len(lefts)), n_mine,
+        jax.ShapeDtypeStruct((8, n_tok, width), F32),
+        route_specs(route, layer, (0, 1, 2, 3), n_mine) + [per_expert(ff)] * len(lefts)
+        + [weight_spec(weights, len(lefts), which)],
+        pl.BlockSpec((8, n_tok, width), lambda i: (0, 0, 0)),
+        [pltpu.VMEM((n_mine, ROWS, width), F32)])(*[route] * 4, *lefts, weights)
 
 
 def solution(mesh):
@@ -603,18 +647,18 @@
         part = expert_combine(route, 0, low[3:], w_first, 2)
         y_low, u_top, u_all = pass_line(part, u_act, w_mix[1], False, True, 2)
 
-        w_top, u_all = lax.optimization_barrier((w_top, u_all))
-        top = expert_forward(route, 1, u_all, w_top)
-        pack, d_gate, d_up = expert_backward(route, 1, tok_all, 1, w_top, *top)
+        recv, grad_in = expert_select(route, 1, u_all, tok_all, 1)
+        w_top, recv = lax.optimization_barrier((w_top, recv))
+        pack, d_gate, d_up, hidden = expert_top(recv, grad_in, w_top)
         grad_top = scatter_grads(pack)
         part = expert_combine(route, 1, (d_gate, d_up), w_top, 0)
         d_u, d_y, dy_all = pass_line(part, d_out, w_mix[1], True, True, 3)
         mix_top = dot('td,te->de', y_low, d_u).astype(BF16)
 
-        pack, d_gate, d_up = expert_backward(route, 0, dy_all, 0, w_first, *low)
+        pack, d_gate, d_up = expert_backward(route, 0, dy_all, w_first, *low)
         grad_low = scatter_grads(pack)
         part_v = expert_combine(route, 0, (d_gate, d_up), w_first, 0)
-        hidden, part_v = lax.optimization_barrier((top[3], part_v))
+        hidden, part_v = lax.optimization_barrier((hidden, part_v))
         part_y = expert_combine(route, 1, (hidden,), w_top, 2)
         d_tokens, layer_out, mix_out = close_line(part_v, d_y, w_mix[0], tokens, mix_top, part_y, u_top, 4)
         grad_top, d_tokens = lax.optimization_barrier((grad_top, d_tokens))

time: 501 us -> 403 us (0.80)
  waiting for transfers between devices: 96.2 us -> 20.9 us
  Pallas kernels: 367 us -> 338 us
  other arithmetic: 6.21 us -> 12.2 us
    reduce_scatter x2, waiting for transfers between devices: 88.7 us -> 12.7 us  [scatter_grads(): lax.psum_scatter(pack.reshape(16 * 3 * n_half * d_model, ff), ('y', 'x'),...]
    pallas_call x8, Pallas kernels: 143 us -> 110 us  [the longest x4 56.5 us: expert_combine(): local_call(functools.partial(combine_kernel, len(lefts)), n_mine, jax.Sha...]
  transfers between devices with their start and end apart: 5 -> 5, of which waited for: 3 -> 3; matrix products, arithmetic and copies ran while one was open for 1% -> 2% of each run, Pallas kernels for 37% -> 62%
where the time goes in v2:
time: 403 us; the launch traced here: 402 us
  Pallas kernels  338 us (84%)
  waiting for transfers between devices  20.9 us (5%)
  between operations  13.9 us (3%)
  local copies, waits for them, and re-layouts  12.5 us (3%)
  other arithmetic  12.2 us (3%)
    pallas_call x2, Pallas kernels, pass_line(): pl.pallas_call(functools.partial(pass_kernel, transpose, want_all), name=...  83.6 us
    pallas_call x1, Pallas kernels, close_line(): pl.pallas_call(close_kernel, name='close_line', out_shape=[block, block,...  73.6 us
    pallas_call x1, Pallas kernels, open_line(): pl.pallas_call(functools.partial(open_kernel, n_chip), name='open_line',...  71 us
    pallas_call x4, Pallas kernels, expert_combine(): local_call(functools.partial(combine_kernel, len(lefts)), n_mine, jax.Sha...  56.5 us
    pallas_call x1, Pallas kernels, expert_top(): local_call(top_kernel, n_mine, [jax.ShapeDtypeStruct(weights.shape, BF16)...  17.9 us
    pallas_call x1, Pallas kernels, expert_backward(): local_call(backward_kernel, n_mine, [jax.ShapeDtypeStruct(weights.shape,...  17.7 us
    reduce_scatter x2, waiting for transfers between devices, scatter_grads(): lax.psum_scatter(pack.reshape(16 * 3 * n_half * d_model, ff), ('y', 'x'),...  12.7 us
    pallas_call x1, Pallas kernels, expert_forward(): local_call(forward_kernel, n_mine, [per_slot(n_mine, width, BF16), per_sl...  9.87 us
  transfers between devices with their start and end apart: 5, of which 3 were waited for; matrix products, arithmetic and copies ran while one was open for 2% of the time, Pallas kernels for 62%

profile of v2, /device:TPU:1, one launch (start us, length us, event | category | flops | bytes accessed | tf_op | source)
XLA Modules:
  0.0 401.6 jit_solution(7542159288369256202)
XLA Ops:
  12.2 1.1 copy.30.base
  13.3 1.2 copy.28
  14.5 2.1 fusion.9
  21.5 71.0 %open_line.1 = (bf16[8,512,448]{2,1,0:T(8,128)(2,1)}, f32[2,4,8,32,256]{4,3,2,1,0:T(8,128)}, bf16[16,3,2,448,128]{4,3,2,1,0:T(8,128)(2,1)}) custom-call(bf16[512,448]{1,0:T(8,128)(2,1)} %pad_maximum_fusion.5.tok_src, bf16[64,256]{1,0:T(8,128)(2,1)} %bitcast.85, bf16[3,2,448,128]{3,2,1,0:T(8,128)(2,1)} %pad_maximum_fusion.4.w_src), custom_call_target="tpu_custom_call" | custom-call | tf_op jit(solution)/shard_map/open_line/pallas_call | solution.py:374
  92.6 9.9 %shard_map.127 = (bf16[32,192,448]{2,1,0:T(8,128)(2,1)}, f32[32,192,128]{2,1,0:T(8,128)}, f32[32,192,128]{2,1,0:T(8,128)}, bf16[32,192,128]{2,1,0:T(8,128)(2,1)}) custom-call(f32[2,4,8,32,256]{4,3,2,1,0:T(8,128)} %get-tuple-element.41.pos.hi.mid.lo, bf16[8,512,448]{2,1,0:T(8,128)(2,1)} %get-tuple-element.42.u_all.dy_all, ...), custom_call_target="tpu_custom_call" | custom-call | tf_op jit(solution)/shard_map/pallas_call | solution.py:549
  102.5 13.5 %shard_map.128.part = f32[8,256,448]{2,1,0:T(8,128)} custom-call(f32[2,4,8,32,256]{4,3,2,1,0:T(8,128)} %get-tuple-element.41.pos.hi.mid.lo, f32[2,4,8,32,256]{4,3,2,1,0:T(8,128)} %get-tuple-element.41.pos.hi.mid.lo, f32[2,4,8,32,256]{4,3,2,1,0:T(8,128)} %get-tuple-element.41.pos.hi.mid.lo, f32[2,4,8,32,256]{4,3,2,1,0:T(8,128)} %get-tuple-element.41.pos.hi.mid.lo, ...), custom_call_target="tpu_custom_call" | custom-call | tf_op jit(solution)/shard_map/pallas_call | solution.py:590
  117.0 41.7 %pass_line.2 = (bf16[256,448]{1,0:T(8,128)(2,1)}, bf16[256,448]{1,0:T(8,128)(2,1)}, bf16[8,256,448]{2,1,0:T(8,128)(2,1)}) custom-call(f32[8,256,448]{2,1,0:T(8,128)} %shard_map.128.part, bf16[256,448]{1,0:T(8,128)(2,1)} %copy-done.1, bf16[448,448]{1,0:T(8,128)(2,1)} %get-tuple-element.101.w_mix), custom_call_target="tpu_custom_call" | custom-call | tf_op jit(solution)/shard_map/pass_line/pallas_call | solution.py:151
  158.7 8.2 %shard_map.129 = (bf16[32,192,448]{2,1,0:T(8,128)(2,1)}, bf16[32,192,448]{2,1,0:T(8,128)(2,1)}) custom-call(f32[2,4,8,32,256]{4,3,2,1,0:T(8,128)} %get-tuple-element.41.pos.hi.mid.lo, f32[2,4,8,32,256]{4,3,2,1,0:T(8,128)} %get-tuple-element.41.pos.hi.mid.lo, f32[2,4,8,32,256]{4,3,2,1,0:T(8,128)} %get-tuple-element.41.pos.hi.mid.lo, ...), custom_call_target="tpu_custom_call" | custom-call | tf_op jit(solution)/shard_map/pallas_call | solution.py:571
  166.9 7.5 %all-gather.2.cloned.1.call-done = bf16[16,2688,128]{2,1,0:T(8,128)(2,1)} async-done(((bf16[1,2688,128]{2,1,0:T(8,128)(2,1)}), bf16[16,2688,128]{2,1,0:T(8,128)(2,1)}) %all-gather.2.cloned.1.call-update) | async-done | bytes 11010064 | tf_op jit(solution)/shard_map/all_gather | solution.py:643
  174.4 17.9 %shard_map.130 = (bf16[16,3,2,448,128]{4,3,2,1,0:T(8,128)(2,1)}, bf16[32,192,128]{2,1,0:T(8,128)(2,1)}, bf16[32,192,128]{2,1,0:T(8,128)(2,1)}, bf16[32,192,128]{2,1,0:T(8,128)(2,1)}) custom-call(bf16[32,192,448]{2,1,0:T(8,128)(2,1)} %get-tuple-element.47.recv, bf16[32,192,448]{2,1,0:T(8,128)(2,1)} %get-tuple-element.48.grad_in, ...), custom_call_target="tpu_custom_call" | custom-call | tf_op jit(solution)/shard_map/pallas_call | solution.py:580
  192.5 14.8 %shard_map.131.part = f32[8,256,448]{2,1,0:T(8,128)} custom-call(f32[2,4,8,32,256]{4,3,2,1,0:T(8,128)} %get-tuple-element.41.pos.hi.mid.lo, f32[2,4,8,32,256]{4,3,2,1,0:T(8,128)} %get-tuple-element.41.pos.hi.mid.lo, f32[2,4,8,32,256]{4,3,2,1,0:T(8,128)} %get-tuple-element.41.pos.hi.mid.lo, f32[2,4,8,32,256]{4,3,2,1,0:T(8,128)} %get-tuple-element.41.pos.hi.mid.lo, ...), custom_call_target="tpu_custom_call" | custom-call | tf_op jit(solution)/shard_map/pallas_call | solution.py:590
  207.3 41.9 %pass_line.3 = (bf16[256,448]{1,0:T(8,128)(2,1)}, bf16[256,448]{1,0:T(8,128)(2,1)}, bf16[8,256,448]{2,1,0:T(8,128)(2,1)}) custom-call(f32[8,256,448]{2,1,0:T(8,128)} %shard_map.131.part, bf16[256,448]{1,0:T(8,128)(2,1)} %copy-done, bf16[448,448]{1,0:T(8,128)(2,1)} %get-tuple-element.101.w_mix), custom_call_target="tpu_custom_call" | custom-call | tf_op jit(solution)/shard_map/pass_line/pallas_call | solution.py:151
  249.2 17.7 %shard_map.132 = (bf16[16,3,2,448,128]{4,3,2,1,0:T(8,128)(2,1)}, bf16[32,192,128]{2,1,0:T(8,128)(2,1)}, bf16[32,192,128]{2,1,0:T(8,128)(2,1)}) custom-call(f32[2,4,8,32,256]{4,3,2,1,0:T(8,128)} %get-tuple-element.41.pos.hi.mid.lo, f32[2,4,8,32,256]{4,3,2,1,0:T(8,128)} %get-tuple-element.41.pos.hi.mid.lo, ...), custom_call_target="tpu_custom_call" | custom-call | tf_op jit(solution)/shard_map/pallas_call | solution.py:559
  267.8 14.8 %shard_map.133.part_v = f32[8,256,448]{2,1,0:T(8,128)} custom-call(f32[2,4,8,32,256]{4,3,2,1,0:T(8,128)} %get-tuple-element.41.pos.hi.mid.lo, f32[2,4,8,32,256]{4,3,2,1,0:T(8,128)} %get-tuple-element.41.pos.hi.mid.lo, f32[2,4,8,32,256]{4,3,2,1,0:T(8,128)} %get-tuple-element.41.pos.hi.mid.lo, f32[2,4,8,32,256]{4,3,2,1,0:T(8,128)} %get-tuple-element.41.pos.hi.mid.lo, ...), custom_call_target="tpu_custom_call" | custom-call | tf_op jit(solution)/shard_map/pallas_call | solution.py:590
  282.6 13.4 %shard_map.134.part_y = f32[8,256,448]{2,1,0:T(8,128)} custom-call(f32[2,4,8,32,256]{4,3,2,1,0:T(8,128)} %get-tuple-element.41.pos.hi.mid.lo, f32[2,4,8,32,256]{4,3,2,1,0:T(8,128)} %get-tuple-element.41.pos.hi.mid.lo, f32[2,4,8,32,256]{4,3,2,1,0:T(8,128)} %get-tuple-element.41.pos.hi.mid.lo, f32[2,4,8,32,256]{4,3,2,1,0:T(8,128)} %get-tuple-element.41.pos.hi.mid.lo, ...), custom_call_target="tpu_custom_call" | custom-call | tf_op jit(solution)/shard_map/pallas_call | solution.py:590
  296.0 1.1 convolution_convert_fusion.mix_top
  297.1 73.6 %close_line.1 = (bf16[256,448]{1,0:T(8,128)(2,1)}, bf16[256,448]{1,0:T(8,128)(2,1)}, bf16[2,448,448]{2,1,0:T(8,128)(2,1)}) custom-call(f32[8,256,448]{2,1,0:T(8,128)} %shard_map.133.part_v, bf16[256,448]{1,0:T(8,128)(2,1)} %get-tuple-element.60.base_v, bf16[448,448]{1,0:T(8,128)(2,1)} %get-tuple-element.100.w_mix, bf16[256,448]{1,0:T(8,128)(2,1)} %copy.32.x_in, ...), custom_call_target="tpu_custom_call" | custom-call | tf_op jit(solution)/shard_map/close_line/pallas_call | solution.py:248
  371.0 1.8 copy.33
  372.8 1.8 copy.34
  374.6 12.7 %reduce-scatter.5.cloned.1.call-done = bf16[2688,128]{1,0:T(8,128)(2,1)} async-done(((bf16[43008,128]{1,0:T(8,128)(2,1)}), bf16[2688,128]{1,0:T(8,128)(2,1)}) %reduce-scatter.5.cloned.1.call-update) | async-done | bytes 688144 | tf_op jit(solution)/shard_map/reduce_scatter | solution.py:622
  387.3 1.6 collective-permute-start
  388.9 1.2 broadcast_select_fusion
  391.1 1.0 pad_maximum_fusion.2
  392.1 1.0 pad_maximum_fusion
  (63 shorter events, 15.2 us)
Async XLA Ops:
  7.2 9.4 %copy-start.7 = (bf16[2,4,448,128]{3,2,1,0:T(8,128)(2,1)S(1)}, bf16[2,4,448,128]{3,2,1,0:T(8,128)(2,1)}, u32[]{:S(2)}) copy-start(bf16[2,4,448,128]{3,2,1,0:T(8,128)(2,1)} %param.14) | copy-start | bytes 2752516
  7.2 167.2 %all-gather.2.cloned.1.call-start = ((), (), s32[]{:S(2)}) async-start(), calls=%async_computation.2 | async-start | bytes 11698176 | tf_op jit(solution)/shard_map/all_gather | solution.py:643
  12.2 5.4 %copy-start.13 = (bf16[256,64]{0,1:T(8,128)(2,1)}, bf16[256,64]{0,1:T(8,128)(2,1)S(1)}, u32[]{:S(2)}) copy-start(bf16[256,64]{0,1:T(8,128)(2,1)S(1)} %constant_dynamic-update-slice_fusion) | copy-start | bytes 98308
  13.3 5.2 %copy-start = (bf16[256,448]{1,0:T(8,128)(2,1)}, bf16[256,448]{1,0:T(8,128)(2,1)S(1)}, u32[]{:S(2)}) copy-start(bf16[256,448]{1,0:T(8,128)(2,1)S(1)} %copy.30.base) | copy-start | bytes 688132
  14.5 3.1 copy-start.8
  16.6 1.5 copy-start.2
  16.6 1.5 copy-start.3
  18.1 1.2 copy-start.6
  18.1 1.2 copy-start.4
  18.2 1.4 copy-start.5
  18.5 2.1 copy-start.1
  92.5 278.2 %reduce-scatter.3.cloned.1.call-start = ((), (), s32[]{:S(2)}) async-start(), calls=%async_computation.3 | async-start | bytes 11698176 | tf_op jit(solution)/shard_map/reduce_scatter | solution.py:622
  192.3 195.0 %reduce-scatter.5.cloned.1.call-start = ((), (), s32[]{:S(2)}) async-start(), calls=%async_computation.4 | async-start | bytes 11698176 | tf_op jit(solution)/shard_map/reduce_scatter | solution.py:622
  282.6 13.4 %copy-start.11 = (bf16[256,448]{1,0:T(8,128)(2,1)S(1)}, bf16[256,448]{1,0:T(8,128)(2,1)}, u32[]{:S(2)}) copy-start(bf16[256,448]{1,0:T(8,128)(2,1)} %get-tuple-element.61) | copy-start | bytes 688132
  282.6 13.4 %copy-start.12 = (bf16[256,448]{1,0:T(8,128)(2,1)S(1)}, bf16[256,448]{1,0:T(8,128)(2,1)}, u32[]{:S(2)}) copy-start(bf16[256,448]{1,0:T(8,128)(2,1)} %get-tuple-element.62) | copy-start | bytes 688132
  370.8 18.1 %collective-permute-start.1 = (bf16[2688,128]{1,0:T(8,128)(2,1)}, bf16[2688,128]{1,0:T(8,128)(2,1)S(1)}, u32[]{:S(2)}, u32[]{:S(2)}) collective-permute-start(bf16[2688,128]{1,0:T(8,128)(2,1)} %reduce-scatter.3.cloned.1.call-done), channel_id=1, source_target_pairs={{0,1},{1,0},{2,3},{3,2},{4,5},{5,4},{6,7},{7,6},{8,9},{9,8},{10,11... | collective-permute-start | bytes 2064392 | tf_op jit(solution)/shard_map/ppermute | solution.py:627
  387.3 3.6 copy-start.10
  387.3 3.6 collective-permute-start
  392.1 2.0 copy-start.9
Sparse Core Ops, SparseCore 0:
  92.7 81.6 all-gather.1
  192.4 90.1 reduce-scatter.2
  286.1 101.1 reduce-scatter.4

commit v3 on v2

--- a/solution.py
+++ b/solution.py
@@ -13,6 +13,10 @@
 VMEM = pl.BlockSpec(memory_space=pltpu.VMEM)
 
 
+def ring(at, step):
+    return lax.rem(at + (step + 4), 4)
+
+
 def enter(peers):
     barrier = pltpu.get_barrier_semaphore()
     for peer in peers:
@@ -29,7 +33,7 @@
 
 def line_peers():
     z, dp = lax.axis_index('z'), lax.axis_index('dp')
-    up, down = {'z': lax.rem(z + 1, 4)}, {'z': lax.rem(z + 3, 4)}
+    up, down = {'z': ring(z, 1)}, {'z': ring(z, -1)}
     return z, dp, up, down, {'dp': 1 - dp}
 
 
@@ -46,8 +50,7 @@
     rows = src.shape[0]
     half = rows // 2
     me = z * 2 + dp
-    below, above = lax.rem(z + 3, 4) * 2 + dp, lax.rem(z + 1, 4) * 2 + dp
-    far = lax.rem(z + 2, 4) * 2 + dp
+    below, above, far = [ring(z, step) * 2 + dp for step in (-1, 1, 2)]
     lo, hi = pl.ds(0, half), pl.ds(half, half)
     go = functools.partial(send, send_sems=send_sems, recv_sems=recv_sems)
     to_up = go(src, dst.at[me], index=base, peer=up)
@@ -80,7 +83,7 @@
     z, dp, up, down, mate = line_peers()
     half = part.shape[1] // 2
     lo, hi = pl.ds(0, half), pl.ds(half, half)
-    order = [lax.rem(z + 2, 4), lax.rem(z + 1, 4), lax.rem(z + 3, 4), z]
+    order = [ring(z, step) for step in (2, 1, -1, 0)]
     go = functools.partial(send, send_sems=send_sems, recv_sems=recv_sems)
     swaps = [go(part.at[zk * 2 + 1 - dp], d_part.at[k], index=base + k, peer=mate) for k, zk in enumerate(order)]
     yield
@@ -158,7 +161,7 @@
 
 def mix_peers():
     at = {axis: lax.axis_index(axis) for axis in 'xyz'}
-    return at, {axis: [{axis: lax.rem(at[axis] + k, 4)} for k in (1, 2, 3)] for axis in 'xyz'}
+    return at, {axis: [{axis: ring(at[axis], k)} for k in (1, 2, 3)] for axis in 'xyz'}
 
 
 def mix_steps(grad, out, bufs, send_sems, recv_sems, base):
@@ -176,7 +179,7 @@
     mine = pl.ds(pl.multiple_of(at['x'] * quarter, quarter), quarter)
     stage = []
     for k in range(3):
-        rows = pl.ds(pl.multiple_of(lax.rem(at['x'] + k + 1, 4) * quarter, quarter), quarter)
+        rows = pl.ds(pl.multiple_of(ring(at['x'], k + 1) * quarter, quarter), quarter)
         stage.append(go(block.at[rows], quarter_in.at[k], index=base + 1 + k, peer=peers['x'][k]))
     copies += [swap] + stage
     yield
@@ -197,7 +200,7 @@
         for coord in range(4):
             term = jnp.zeros_like(terms[0])
             for k in range(4):
-                source = lax.rem(here + 4 - k, 4)
+                source = ring(here, -k)
                 term = jnp.where(source == coord, terms[k], term)
             total = term if total is None else total + term
     final = total.astype(BF16)
@@ -257,6 +260,8 @@
 
 
 N_PLANE = 40
+WAYS = (1, -1)
+HALVES = (0, 1)
 
 
 def plane_gather_steps(src, dst, send_sems, recv_sems, base):
@@ -268,11 +273,11 @@
 
     def block(half, i, j):
         dx, dy = (i, j) if half == 0 else (j, i)
-        return lax.rem(at['y'] + dy + 4, 4) * 4 + lax.rem(at['x'] + dx + 4, 4)
+        return ring(at['y'], dy) * 4 + ring(at['x'], dx)
 
     def peer(half, stage, step):
         axis = 'xy'[stage] if half == 0 else 'yx'[stage]
-        return {axis: lax.rem(at[axis] + step + 4, 4)}
+        return {axis: ring(at[axis], step)}
 
     counter = [base]
 
@@ -285,33 +290,33 @@
         return copy
 
     first, second, relay1, relay2 = {}, {}, {}, {}
-    for half in (0, 1):
-        for step in (1, -1):
+    for half in HALVES:
+        for step in WAYS:
             first[half, step] = launch(half, 0, step, 0, 0, own=True)
-    for half in (0, 1):
-        for step in (1, -1):
+    for half in HALVES:
+        for step in WAYS:
             second[half, 0, step] = launch(half, 1, step, 0, 0, own=True)
     dst[at['y'] * 4 + at['x']] = src[...]
     yield
-    for step in (1, -1):
-        for half in (0, 1):
+    for step in WAYS:
+        for half in HALVES:
             first[half, step].wait_recv()
             relay1[half, step] = launch(half, 0, step, -step, 0, rows_of=0 if step == 1 else 1)
-            for out in (1, -1):
+            for out in WAYS:
                 second[half, -step, out] = launch(half, 1, out, -step, 0)
     yield
 
     def forward(i):
-        for step in (1, -1):
-            for half in (0, 1):
+        for step in WAYS:
+            for half in HALVES:
                 second[half, i, step].wait_recv()
                 relay2[half, i, step] = launch(half, 1, step, i, -step, rows_of=0 if step == 1 else 1)
 
     forward(0)
-    for half in (0, 1):
-        for step in (1, -1):
+    for half in HALVES:
+        for step in WAYS:
             relay1[half, step].wait_recv()
-        for out in (1, -1):
+        for out in WAYS:
             second[half, 2, out] = launch(half, 1, out, 2, 0)
     yield
     forward(-1)
@@ -324,16 +329,44 @@
     yield
 
 
-def open_kernel(n_chip, tok_src, route_src, w_src, tok_all, route, w_all, route_all, send_sems, recv_sems):
-    z, dp, up, down, mate = line_peers()
+def open_kernel(n_chip, tokens, d_out, w_mix, ids, hi, mid, lo, w_gate, w_up, w_down,
+                tok_all, route, w_all, w_top, u_ref,
+                tok_src, route_src, w_src, route_all, load_sems, send_sems, recv_sems):
+    z, dp, up, down_peer, mate = line_peers()
     at = {axis: lax.axis_index(axis) for axis in 'xy'}
-    enter([up, down, mate] + [{axis: lax.rem(at[axis] + k, 4)} for axis in 'xy' for k in (1, 3)])
+    n_half = n_chip // 2
+    own = pl.ds(dp * n_half, n_half)
+    loads = []
+    for layer, dst in enumerate((w_src, w_top)):
+        for k, (src, to) in enumerate(((w_gate, dst.at[0]), (w_up, dst.at[1]), (w_down, dst.at[2]))):
+            loads.append(pltpu.make_async_copy(src.at[layer, own], to, load_sems.at[layer, k]))
+    for load in loads:
+        load.start()
+    enter([up, down_peer, mate] + [{axis: ring(at[axis], k)} for axis in 'xy' for k in WAYS])
+
+    def unit(size):
+        row = lax.broadcasted_iota(jnp.int32, (size, size), 0)
+        col = lax.broadcasted_iota(jnp.int32, (size, size), 1)
+        return jnp.where(row == col, 1.0, 0.0).astype(BF16)
+
+    for load in loads[:3]:
+        load.wait()
     steps_w = plane_gather_steps(w_src, w_all, send_sems, recv_sems, 0)
     steps_r = line_gather_steps(route_src, route_all, send_sems, recv_sems, N_PLANE)
     steps_t = line_gather_steps(tok_src, tok_all, send_sems, recv_sems, N_PLANE + N_AG)
     next(steps_w)
+    width, tok = tokens.shape
+    columns = [ref[layer] for layer in range(route.shape[0]) for ref in (ids, hi, mid, lo)]
+    route_src[...] = jnp.concatenate(columns, axis=0).astype(BF16)
     next(steps_r)
+    same = unit(width)
+    u = (tn(tokens[...], same) + tn(tokens[...], w_mix[0])).astype(BF16)
+    u_ref[...] = u
+    tok_src[:tok] = u
+    tok_src[tok:] = tn(d_out[...], same).astype(BF16)
     next(steps_t)
+    for load in loads[3:]:
+        load.wait()
     for steps in (steps_r, steps_w, steps_t):
         next(steps)
     next(steps_w)
@@ -341,7 +374,6 @@
         for _ in steps:
             pass
     n_layers, _, _, n_mine, n_tok = route.shape
-    n_half = n_chip // 2
     loc = lax.broadcasted_iota(jnp.int32, (n_mine, n_tok), 0)
     mine = ((z * 16 + loc // n_half) * n_chip + dp * n_half + lax.rem(loc, n_half)).astype(F32)
     row = lax.broadcasted_iota(jnp.int32, (n_tok, n_tok), 0)
@@ -367,19 +399,26 @@
         pass
 
 
-def open_line(tok_src, route_src, w_src, n_layers, n_chip, collective_id):
-    n_tok = route_src.shape[1]
-    n_mine = 16 * n_chip // 2
+def open_line(tokens, d_out, w_mix, routing, w_gate, w_up, w_down, collective_id):
+    width, tok = tokens.shape
+    n_layers, n_chip, _, ff = w_gate.shape
+    n_half = n_chip // 2
+    n_rows = 4 * n_layers * routing[0].shape[1]
     n_sem = N_PLANE + 2 * N_AG
+    own = (3, n_half, width, ff)
+    anywhere = pl.BlockSpec(memory_space=pl.ANY)
     return pl.pallas_call(
         functools.partial(open_kernel, n_chip), name='open_line',
-        out_shape=[jax.ShapeDtypeStruct((8,) + tok_src.shape, BF16),
-                   jax.ShapeDtypeStruct((n_layers, 4, 8, n_mine, n_tok), F32),
-                   jax.ShapeDtypeStruct((16,) + w_src.shape, BF16)],
-        in_specs=[VMEM] * 3, out_specs=[VMEM] * 3,
-        scratch_shapes=[pltpu.VMEM((8,) + route_src.shape, BF16),
+        out_shape=[jax.ShapeDtypeStruct((8, 2 * tok, width), BF16),
+                   jax.ShapeDtypeStruct((n_layers, 4, 8, 16 * n_half, tok), F32),
+                   jax.ShapeDtypeStruct((16,) + own, BF16), jax.ShapeDtypeStruct(own, BF16),
+                   jax.ShapeDtypeStruct((tok, width), BF16)],
+        in_specs=[VMEM] * 7 + [anywhere] * 3, out_specs=[VMEM] * 5,
+        scratch_shapes=[pltpu.VMEM((2 * tok, width), BF16), pltpu.VMEM((n_rows, tok), BF16), pltpu.VMEM(own, BF16),
+                        pltpu.VMEM((8, n_rows, tok), BF16),
+                        pltpu.SemaphoreType.DMA((n_layers, 3)),
                         pltpu.SemaphoreType.DMA((n_sem,)), pltpu.SemaphoreType.DMA((n_sem,))],
-        compiler_params=params(collective_id))(tok_src, route_src, w_src)
+        compiler_params=params(collective_id))(tokens, d_out, w_mix, *routing, w_gate, w_up, w_down)
 
 
 def silu_parts(pre_gate):
@@ -399,6 +438,7 @@
 
 
 CHUNK = 8
+TOP_CHUNK = 4
 SLOT = 24
 ROWS = 8 * SLOT
 
@@ -487,7 +527,7 @@
 
 
 def top_kernel(recv, grad_in, w_all, pack, d_gate, d_up, hidden):
-    for e in range(CHUNK):
+    for e in range(TOP_CHUNK):
         rows = recv[e]
         a, b, h = hidden_of(rows, w_all, e)
         hidden[e] = h
@@ -525,17 +565,17 @@
     return pl.BlockSpec((8, n_tok, tok_all.shape[2]), lambda i: (0, part, 0))
 
 
-def per_expert(last):
-    return pl.BlockSpec((CHUNK, ROWS, last), lambda i: (i, 0, 0))
-
-
-def weight_spec(weights, kinds, first):
-    return pl.BlockSpec((CHUNK // 2, kinds, 2) + weights.shape[3:], lambda i: (i, first // kinds, 0, 0, 0))
-
-
-def local_call(kernel, n_mine, outs, in_specs, out_specs, scratch=()):
+def per_expert(last, chunk=CHUNK):
+    return pl.BlockSpec((chunk, ROWS, last), lambda i: (i, 0, 0))
+
+
+def weight_spec(weights, kinds, first, chunk=CHUNK):
+    return pl.BlockSpec((chunk // 2, kinds, 2) + weights.shape[3:], lambda i: (i, first // kinds, 0, 0, 0))
+
+
+def local_call(kernel, n_mine, outs, in_specs, out_specs, scratch=(), chunk=CHUNK):
     return pl.pallas_call(
-        kernel, grid=(n_mine // CHUNK,), out_shape=outs, in_specs=in_specs, out_specs=out_specs,
+        kernel, grid=(n_mine // chunk,), out_shape=outs, in_specs=in_specs, out_specs=out_specs,
         scratch_shapes=list(scratch), compiler_params=pltpu.CompilerParams(vmem_limit_bytes=60 * 1024 * 1024))
 
 
@@ -559,7 +599,7 @@
     return local_call(
         backward_kernel, n_mine,
         [jax.ShapeDtypeStruct(weights.shape, BF16), per_slot(n_mine, ff, BF16), per_slot(n_mine, ff, BF16)],
-        route_specs(route, layer, (0, 1, 2, 3)) + [token_spec(dy_all, n_tok, 0), weight_spec(weights, 1, 2),
+        route_specs(route, layer, range(4)) + [token_spec(dy_all, n_tok, 0), weight_spec(weights, 1, 2),
                                                    per_expert(width), per_expert(ff), per_expert(ff), per_expert(ff)],
         [weight_spec(weights, 3, 0), per_expert(ff), per_expert(ff)],
         [pltpu.VMEM((CHUNK, ROWS, width), BF16)])(*[route] * 4, dy_all, weights, recv, pre_gate, pre_up, hidden)
@@ -570,7 +610,7 @@
     width = u_all.shape[2]
     return local_call(
         select_kernel, n_mine, [per_slot(n_mine, width, BF16)] * 2,
-        route_specs(route, layer, (0, 1, 2, 3)) + [token_spec(u_all, n_tok, 0), token_spec(dy_all, n_tok, dy_part)],
+        route_specs(route, layer, range(4)) + [token_spec(u_all, n_tok, 0), token_spec(dy_all, n_tok, dy_part)],
         [per_expert(width)] * 2)(*[route] * 4, u_all, dy_all)
 
 
@@ -580,8 +620,9 @@
     return local_call(
         top_kernel, n_mine,
         [jax.ShapeDtypeStruct(weights.shape, BF16)] + [per_slot(n_mine, ff, BF16)] * 3,
-        [per_expert(width)] * 2 + [weight_spec(weights, 3, 0)],
-        [weight_spec(weights, 3, 0)] + [per_expert(ff)] * 3)(recv, grad_in, weights)
+        [per_expert(width, TOP_CHUNK)] * 2 + [weight_spec(weights, 3, 0, TOP_CHUNK)],
+        [weight_spec(weights, 3, 0, TOP_CHUNK)] + [per_expert(ff, TOP_CHUNK)] * 3, chunk=TOP_CHUNK)(
+            recv, grad_in, weights)
 
 
 def expert_combine(route, layer, lefts, weights, which):
@@ -590,7 +631,7 @@
     return local_call(
         functools.partial(combine_kernel, len(lefts)), n_mine,
         jax.ShapeDtypeStruct((8, n_tok, width), F32),
-        route_specs(route, layer, (0, 1, 2, 3), n_mine) + [per_expert(ff)] * len(lefts)
+        route_specs(route, layer, range(4), n_mine) + [per_expert(ff)] * len(lefts)
         + [weight_spec(weights, len(lefts), which)],
         pl.BlockSpec((8, n_tok, width), lambda i: (0, 0, 0)),
         [pltpu.VMEM((n_mine, ROWS, width), F32)])(*[route] * 4, *lefts, weights)
@@ -605,18 +646,11 @@
     expert_spec = P(None, ep, None, None)
 
     def device_body(tokens, d_out, expert_ids, gate_vals, w_mix, w_gate, w_up, w_down):
-        n_layers = w_mix.shape[0]
         n_chip = w_gate.shape[1]
         n_half = n_chip // 2
         _, d_model = tokens.shape
         ff = w_gate.shape[3]
         dp = lax.axis_index('dp')
-
-        def own_weights(layer):
-            wg = lax.dynamic_slice_in_dim(w_gate[layer], dp * n_half, n_half, 0)
-            wu = lax.dynamic_slice_in_dim(w_up[layer], dp * n_half, n_half, 0)
-            wd = lax.dynamic_slice_in_dim(w_down[layer], dp * n_half, n_half, 0)
-            return jnp.stack([wg, wu, jnp.swapaxes(wd, 1, 2)], axis=0)
 
         def scatter_grads(pack):
             part = lax.psum_scatter(pack.reshape(16 * 3 * n_half * d_model, ff), ('y', 'x'),
@@ -630,16 +664,9 @@
             both = jnp.concatenate([lo, hi], axis=1)
             return both[0], both[1], jnp.swapaxes(both[2], 1, 2)
 
-        route_src = []
-        for layer in range(n_layers):
-            route_src.append(expert_ids[layer].astype(BF16))
-            route_src.extend(part.astype(BF16) for part in split3(gate_vals[layer]))
-        route_src = jnp.concatenate(route_src, axis=1).T
-
-        u_act = (tokens.astype(F32) + dot('td,de->te', tokens, w_mix[0])).astype(BF16)
-        first = jnp.concatenate([u_act, d_out], axis=0)
-        tok_all, route, w_first = open_line(first, route_src, own_weights(0), n_layers, n_chip, 1)
-        own_top, w_first = lax.optimization_barrier((own_weights(1), w_first))
+        routing = [jnp.swapaxes(expert_ids, 1, 2).astype(F32)] + list(split3(jnp.swapaxes(gate_vals, 1, 2)))
+        tok_all, route, w_first, own_top, u_act = open_line(tokens.T, d_out.T, w_mix, routing, w_gate, w_up,
+                                                            jnp.swapaxes(w_down, 2, 3), 1)
         w_top = lax.all_gather(own_top.reshape(3 * n_half * d_model, ff), ('y', 'x'), axis=0, tiled=False)
         w_top = w_top.reshape(16, 3, n_half, d_model, ff)
 

time: 403 us -> 395 us (0.980)
  other arithmetic: 12.2 us -> 7.4 us
  transfers between devices with their start and end apart: 5 -> 5, of which waited for: 3 -> 2; matrix products, arithmetic and copies ran while one was open for 2% -> 2% of each run, Pallas kernels for 62% -> 63%
where the time goes in v3:
time: 395 us; the launch traced here: 394 us
  Pallas kernels  338 us (86%)
  waiting for transfers between devices  22.7 us (6%)
  between operations  13.8 us (3%)
  local copies, waits for them, and re-layouts  8.73 us (2%)
  other arithmetic  7.4 us (2%)
    pallas_call x2, Pallas kernels, pass_line(): pl.pallas_call(functools.partial(pass_kernel, transpose, want_all), name=...  83.7 us
    pallas_call x1, Pallas kernels, close_line(): pl.pallas_call(close_kernel, name='close_line', out_shape=[block, block,...  72 us
    pallas_call x1, Pallas kernels, open_line(): pl.pallas_call(functools.partial(open_kernel, n_chip), name='open_line',...  71.5 us
    pallas_call x4, Pallas kernels, expert_combine(): local_call(functools.partial(combine_kernel, len(lefts)), n_mine, jax.Sha...  56.3 us
    pallas_call x1, Pallas kernels, expert_top(): local_call(top_kernel, n_mine, [jax.ShapeDtypeStruct(weights.shape, BF16)...  18.6 us
    pallas_call x1, Pallas kernels, expert_backward(): local_call(backward_kernel, n_mine, [jax.ShapeDtypeStruct(weights.shape,...  17.7 us
    reduce_scatter x2, waiting for transfers between devices, scatter_grads(): lax.psum_scatter(pack.reshape(16 * 3 * n_half * d_model, ff), ('y', 'x'),...  15.3 us
    pallas_call x1, Pallas kernels, expert_forward(): local_call(forward_kernel, n_mine, [per_slot(n_mine, width, BF16), per_sl...  9.82 us
  transfers between devices with their start and end apart: 5, of which 2 were waited for; matrix products, arithmetic and copies ran while one was open for 2% of the time, Pallas kernels for 63%

profile of v3, /device:TPU:1, one launch (start us, length us, event | category | flops | bytes accessed | tf_op | source)
XLA Modules:
  0.0 393.7 jit_solution(2053138554425904120)
XLA Ops:
  7.2 1.3 convert_bitcast_fusion.ids
  8.5 1.3 fusion.6
  9.9 71.5 %open_line.1 = (bf16[8,512,448]{2,1,0:T(8,128)(2,1)}, f32[2,4,8,32,256]{4,3,2,1,0:T(8,128)}, bf16[16,3,2,448,128]{4,3,2,1,0:T(8,128)(2,1)}, bf16[3,2,448,128]{3,2,1,0:T(8,128)(2,1)}, bf16[256,448]{1,0:T(8,128)(2,1)}) custom-call(bf16[448,256]{1,0:T(8,128)(2,1)} %bitcast.52, bf16[448,256]{1,0:T(8,128)(2,1)} %bitcast.51, bf16[2,448,448]{2,1,0:T(8,128)(2,1)} %w_mix.1, ...), custom_call_target="tpu_custom_call" | custom-call | tf_op jit(solution)/shard_map/open_line/pallas_call | solution.py:410
  81.5 9.8 %shard_map.127 = (bf16[32,192,448]{2,1,0:T(8,128)(2,1)}, f32[32,192,128]{2,1,0:T(8,128)}, f32[32,192,128]{2,1,0:T(8,128)}, bf16[32,192,128]{2,1,0:T(8,128)(2,1)}) custom-call(f32[2,4,8,32,256]{4,3,2,1,0:T(8,128)} %get-tuple-element.40.pos.hi.mid.lo, bf16[8,512,448]{2,1,0:T(8,128)(2,1)} %get-tuple-element.41.u_all.dy_all, ...), custom_call_target="tpu_custom_call" | custom-call | tf_op jit(solution)/shard_map/pallas_call | solution.py:589
  91.3 13.6 %shard_map.128.part = f32[8,256,448]{2,1,0:T(8,128)} custom-call(f32[2,4,8,32,256]{4,3,2,1,0:T(8,128)} %get-tuple-element.40.pos.hi.mid.lo, f32[2,4,8,32,256]{4,3,2,1,0:T(8,128)} %get-tuple-element.40.pos.hi.mid.lo, f32[2,4,8,32,256]{4,3,2,1,0:T(8,128)} %get-tuple-element.40.pos.hi.mid.lo, f32[2,4,8,32,256]{4,3,2,1,0:T(8,128)} %get-tuple-element.40.pos.hi.mid.lo, ...), custom_call_target="tpu_custom_call" | custom-call | tf_op jit(solution)/shard_map/pallas_call | solution.py:631
  105.8 41.7 %pass_line.2 = (bf16[256,448]{1,0:T(8,128)(2,1)}, bf16[256,448]{1,0:T(8,128)(2,1)}, bf16[8,256,448]{2,1,0:T(8,128)(2,1)}) custom-call(f32[8,256,448]{2,1,0:T(8,128)} %shard_map.128.part, bf16[256,448]{1,0:T(8,128)(2,1)} %get-tuple-element.44.base, bf16[448,448]{1,0:T(8,128)(2,1)} %get-tuple-element.95.w_mix), custom_call_target="tpu_custom_call" | custom-call | tf_op jit(solution)/shard_map/pass_line/pallas_call | solution.py:154
  147.5 8.3 %shard_map.129 = (bf16[32,192,448]{2,1,0:T(8,128)(2,1)}, bf16[32,192,448]{2,1,0:T(8,128)(2,1)}) custom-call(f32[2,4,8,32,256]{4,3,2,1,0:T(8,128)} %get-tuple-element.40.pos.hi.mid.lo, f32[2,4,8,32,256]{4,3,2,1,0:T(8,128)} %get-tuple-element.40.pos.hi.mid.lo, f32[2,4,8,32,256]{4,3,2,1,0:T(8,128)} %get-tuple-element.40.pos.hi.mid.lo, ...), custom_call_target="tpu_custom_call" | custom-call | tf_op jit(solution)/shard_map/pallas_call | solution.py:611
  155.8 7.4 %all-gather.2.cloned.1.call-done = bf16[16,2688,128]{2,1,0:T(8,128)(2,1)} async-done(((bf16[1,2688,128]{2,1,0:T(8,128)(2,1)}), bf16[16,2688,128]{2,1,0:T(8,128)(2,1)}) %all-gather.2.cloned.1.call-update) | async-done | bytes 11010064 | tf_op jit(solution)/shard_map/all_gather | solution.py:670
  163.2 18.6 %shard_map.130 = (bf16[16,3,2,448,128]{4,3,2,1,0:T(8,128)(2,1)}, bf16[32,192,128]{2,1,0:T(8,128)(2,1)}, bf16[32,192,128]{2,1,0:T(8,128)(2,1)}, bf16[32,192,128]{2,1,0:T(8,128)(2,1)}) custom-call(bf16[32,192,448]{2,1,0:T(8,128)(2,1)} %get-tuple-element.47.recv, bf16[32,192,448]{2,1,0:T(8,128)(2,1)} %get-tuple-element.48.grad_in, ...), custom_call_target="tpu_custom_call" | custom-call | tf_op jit(solution)/shard_map/pallas_call | solution.py:620
  183.6 14.6 %shard_map.131.part = f32[8,256,448]{2,1,0:T(8,128)} custom-call(f32[2,4,8,32,256]{4,3,2,1,0:T(8,128)} %get-tuple-element.40.pos.hi.mid.lo, f32[2,4,8,32,256]{4,3,2,1,0:T(8,128)} %get-tuple-element.40.pos.hi.mid.lo, f32[2,4,8,32,256]{4,3,2,1,0:T(8,128)} %get-tuple-element.40.pos.hi.mid.lo, f32[2,4,8,32,256]{4,3,2,1,0:T(8,128)} %get-tuple-element.40.pos.hi.mid.lo, ...), custom_call_target="tpu_custom_call" | custom-call | tf_op jit(solution)/shard_map/pallas_call | solution.py:631
  198.2 42.1 %pass_line.3 = (bf16[256,448]{1,0:T(8,128)(2,1)}, bf16[256,448]{1,0:T(8,128)(2,1)}, bf16[8,256,448]{2,1,0:T(8,128)(2,1)}) custom-call(f32[8,256,448]{2,1,0:T(8,128)} %shard_map.131.part, bf16[256,448]{1,0:T(8,128)(2,1)} %copy.18.base, bf16[448,448]{1,0:T(8,128)(2,1)} %get-tuple-element.95.w_mix), custom_call_target="tpu_custom_call" | custom-call | tf_op jit(solution)/shard_map/pass_line/pallas_call | solution.py:154
  240.3 17.7 %shard_map.132 = (bf16[16,3,2,448,128]{4,3,2,1,0:T(8,128)(2,1)}, bf16[32,192,128]{2,1,0:T(8,128)(2,1)}, bf16[32,192,128]{2,1,0:T(8,128)(2,1)}) custom-call(f32[2,4,8,32,256]{4,3,2,1,0:T(8,128)} %get-tuple-element.40.pos.hi.mid.lo, f32[2,4,8,32,256]{4,3,2,1,0:T(8,128)} %get-tuple-element.40.pos.hi.mid.lo, ...), custom_call_target="tpu_custom_call" | custom-call | tf_op jit(solution)/shard_map/pallas_call | solution.py:599
  259.7 14.8 %shard_map.133.part_v = f32[8,256,448]{2,1,0:T(8,128)} custom-call(f32[2,4,8,32,256]{4,3,2,1,0:T(8,128)} %get-tuple-element.40.pos.hi.mid.lo, f32[2,4,8,32,256]{4,3,2,1,0:T(8,128)} %get-tuple-element.40.pos.hi.mid.lo, f32[2,4,8,32,256]{4,3,2,1,0:T(8,128)} %get-tuple-element.40.pos.hi.mid.lo, f32[2,4,8,32,256]{4,3,2,1,0:T(8,128)} %get-tuple-element.40.pos.hi.mid.lo, ...), custom_call_target="tpu_custom_call" | custom-call | tf_op jit(solution)/shard_map/pallas_call | solution.py:631
  274.5 13.3 %shard_map.134.part_y = f32[8,256,448]{2,1,0:T(8,128)} custom-call(f32[2,4,8,32,256]{4,3,2,1,0:T(8,128)} %get-tuple-element.40.pos.hi.mid.lo, f32[2,4,8,32,256]{4,3,2,1,0:T(8,128)} %get-tuple-element.40.pos.hi.mid.lo, f32[2,4,8,32,256]{4,3,2,1,0:T(8,128)} %get-tuple-element.40.pos.hi.mid.lo, f32[2,4,8,32,256]{4,3,2,1,0:T(8,128)} %get-tuple-element.40.pos.hi.mid.lo, ...), custom_call_target="tpu_custom_call" | custom-call | tf_op jit(solution)/shard_map/pallas_call | solution.py:631
  287.8 1.1 convolution_convert_fusion.mix_top
  288.8 72.0 %close_line.1 = (bf16[256,448]{1,0:T(8,128)(2,1)}, bf16[256,448]{1,0:T(8,128)(2,1)}, bf16[2,448,448]{2,1,0:T(8,128)(2,1)}) custom-call(f32[8,256,448]{2,1,0:T(8,128)} %shard_map.133.part_v, bf16[256,448]{1,0:T(8,128)(2,1)} %get-tuple-element.60.base_v, bf16[448,448]{1,0:T(8,128)(2,1)} %get-tuple-element.94.w_mix, bf16[256,448]{1,0:T(8,128)(2,1)} %copy.19.x_in, ...), custom_call_target="tpu_custom_call" | custom-call | tf_op jit(solution)/shard_map/close_line/pallas_call | solution.py:251
  361.0 15.2 %reduce-scatter.5.cloned.1.call-done = bf16[2688,128]{1,0:T(8,128)(2,1)} async-done(((bf16[43008,128]{1,0:T(8,128)(2,1)}), bf16[2688,128]{1,0:T(8,128)(2,1)}) %reduce-scatter.5.cloned.1.call-update) | async-done | bytes 688144 | tf_op jit(solution)/shard_map/reduce_scatter | solution.py:656
  376.3 1.7 collective-permute-start
  378.0 1.8 copy.20
  379.7 1.8 copy.21
  381.5 1.5 broadcast_select_fusion
  383.3 1.0 pad_maximum_fusion.2
  384.3 1.0 pad_maximum_fusion
  385.3 1.0 pad_maximum_fusion.1
  (28 shorter events, 6.0 us)
Async XLA Ops:
  7.2 156.0 %all-gather.2.cloned.1.call-start = ((), (), s32[]{:S(2)}) async-start(), calls=%async_computation.2 | async-start | bytes 11698176 | tf_op jit(solution)/shard_map/all_gather | solution.py:670
  81.4 279.4 %reduce-scatter.3.cloned.1.call-start = ((), (), s32[]{:S(2)}) async-start(), calls=%async_computation.3 | async-start | bytes 11698176 | tf_op jit(solution)/shard_map/reduce_scatter | solution.py:656
  91.3 13.6 %copy-start = (bf16[2,448,448]{2,1,0:T(8,128)(2,1)S(1)}, bf16[2,448,448]{2,1,0:T(8,128)(2,1)}, u32[]{:S(2)}) copy-start(bf16[2,448,448]{2,1,0:T(8,128)(2,1)} %w_mix.1) | copy-start | bytes 2408452
  181.8 0.9 copy-start.2
  181.8 194.5 %reduce-scatter.5.cloned.1.call-start = ((), (), s32[]{:S(2)}) async-start(), calls=%async_computation.4 | async-start | bytes 11698176 | tf_op jit(solution)/shard_map/reduce_scatter | solution.py:656
  257.9 0.9 copy-start.3
  274.5 13.3 %copy-start.4 = (bf16[256,448]{1,0:T(8,128)(2,1)S(1)}, bf16[256,448]{1,0:T(8,128)(2,1)}, u32[]{:S(2)}) copy-start(bf16[256,448]{1,0:T(8,128)(2,1)} %get-tuple-element.61) | copy-start | bytes 688132
  274.5 13.3 %copy-start.5 = (bf16[256,448]{1,0:T(8,128)(2,1)S(1)}, bf16[256,448]{1,0:T(8,128)(2,1)}, u32[]{:S(2)}) copy-start(bf16[256,448]{1,0:T(8,128)(2,1)} %get-tuple-element.62) | copy-start | bytes 688132
  360.9 20.7 %collective-permute-start.1 = (bf16[2688,128]{1,0:T(8,128)(2,1)}, bf16[2688,128]{1,0:T(8,128)(2,1)S(1)}, u32[]{:S(2)}, u32[]{:S(2)}) collective-permute-start(bf16[2688,128]{1,0:T(8,128)(2,1)} %reduce-scatter.3.cloned.1.call-done), channel_id=1, source_target_pairs={{0,1},{1,0},{2,3},{3,2},{4,5},{5,4},{6,7},{7,6},{8,9},{9,8},{10,11... | collective-permute-start | bytes 2064392 | tf_op jit(solution)/shard_map/ppermute | solution.py:661
  376.3 5.2 %collective-permute-start = (bf16[2688,128]{1,0:T(8,128)(2,1)}, bf16[2688,128]{1,0:T(8,128)(2,1)S(1)}, u32[]{:S(2)}, u32[]{:S(2)}) collective-permute-start(bf16[2688,128]{1,0:T(8,128)(2,1)} %reduce-scatter.5.cloned.1.call-done), channel_id=1, source_target_pairs={{0,1},{1,0},{2,3},{3,2},{4,5},{5,4},{6,7},{7,6},{8,9},{9,8},{10,11... | collective-permute-start | bytes 2064392 | tf_op jit(solution)/shard_map/ppermute | solution.py:661
  384.3 2.0 copy-start.1
Sparse Core Ops, SparseCore 0:
  81.5 81.6 all-gather.1
  181.9 90.0 reduce-scatter.2
  275.5 100.7 reduce-scatter.4

commit v4 on v3

--- a/solution.py
+++ b/solution.py
@@ -236,18 +236,19 @@
     d_u = (base_v[...].astype(F32) + next(steps_v)).astype(BF16)
     grad[0] = tn(x_in[...], d_u).astype(BF16)
     next(steps_m)
-    dx_ref[...] = (d_u.astype(F32) + nt(d_u, w_mix[...])).astype(BF16)
+    same = unit(d_u.shape[1])
+    dx_ref[...] = nt(same, (d_u.astype(F32) + nt(d_u, w_mix[...])).astype(BF16)).astype(BF16)
     next(steps_m)
     next(steps_y)
     next(steps_m)
-    y_ref[...] = (base_y[...].astype(F32) + next(steps_y)).astype(BF16)
+    y_ref[...] = nt(same, (base_y[...].astype(F32) + next(steps_y)).astype(BF16)).astype(BF16)
 
 
 def close_line(part_v, base_v, w_mix, x_in, mix_top, part_y, base_y, collective_id):
     _, tok, width = part_v.shape
     quarter = width // 4
     n_sem = 2 * N_RS + N_MIX
-    block = jax.ShapeDtypeStruct((tok, width), BF16)
+    block = jax.ShapeDtypeStruct((width, tok), BF16)
     return pl.pallas_call(
         close_kernel, name='close_line',
         out_shape=[block, block, jax.ShapeDtypeStruct((2, width, width), BF16)],
@@ -329,7 +330,7 @@
     yield
 
 
-def open_kernel(n_chip, tokens, d_out, w_mix, ids, hi, mid, lo, w_gate, w_up, w_down,
+def open_kernel(n_chip, tokens, d_out, w_mix, ids, gates, w_gate, w_up, w_down,
                 tok_all, route, w_all, w_top, u_ref,
                 tok_src, route_src, w_src, route_all, load_sems, send_sems, recv_sems):
     z, dp, up, down_peer, mate = line_peers()
@@ -343,12 +344,6 @@
     for load in loads:
         load.start()
     enter([up, down_peer, mate] + [{axis: ring(at[axis], k)} for axis in 'xy' for k in WAYS])
-
-    def unit(size):
-        row = lax.broadcasted_iota(jnp.int32, (size, size), 0)
-        col = lax.broadcasted_iota(jnp.int32, (size, size), 1)
-        return jnp.where(row == col, 1.0, 0.0).astype(BF16)
-
     for load in loads[:3]:
         load.wait()
     steps_w = plane_gather_steps(w_src, w_all, send_sems, recv_sems, 0)
@@ -356,7 +351,9 @@
     steps_t = line_gather_steps(tok_src, tok_all, send_sems, recv_sems, N_PLANE + N_AG)
     next(steps_w)
     width, tok = tokens.shape
-    columns = [ref[layer] for layer in range(route.shape[0]) for ref in (ids, hi, mid, lo)]
+    columns = []
+    for layer in range(route.shape[0]):
+        columns += [ids[layer].astype(F32), *split3(gates[layer])]
     route_src[...] = jnp.concatenate(columns, axis=0).astype(BF16)
     next(steps_r)
     same = unit(width)
@@ -399,11 +396,11 @@
         pass
 
 
-def open_line(tokens, d_out, w_mix, routing, w_gate, w_up, w_down, collective_id):
+def open_line(tokens, d_out, w_mix, ids, gates, w_gate, w_up, w_down, collective_id):
     width, tok = tokens.shape
     n_layers, n_chip, _, ff = w_gate.shape
     n_half = n_chip // 2
-    n_rows = 4 * n_layers * routing[0].shape[1]
+    n_rows = 4 * n_layers * ids.shape[1]
     n_sem = N_PLANE + 2 * N_AG
     own = (3, n_half, width, ff)
     anywhere = pl.BlockSpec(memory_space=pl.ANY)
@@ -413,12 +410,12 @@
                    jax.ShapeDtypeStruct((n_layers, 4, 8, 16 * n_half, tok), F32),
                    jax.ShapeDtypeStruct((16,) + own, BF16), jax.ShapeDtypeStruct(own, BF16),
                    jax.ShapeDtypeStruct((tok, width), BF16)],
-        in_specs=[VMEM] * 7 + [anywhere] * 3, out_specs=[VMEM] * 5,
+        in_specs=[VMEM] * 5 + [anywhere] * 3, out_specs=[VMEM] * 5,
         scratch_shapes=[pltpu.VMEM((2 * tok, width), BF16), pltpu.VMEM((n_rows, tok), BF16), pltpu.VMEM(own, BF16),
                         pltpu.VMEM((8, n_rows, tok), BF16),
                         pltpu.SemaphoreType.DMA((n_layers, 3)),
                         pltpu.SemaphoreType.DMA((n_sem,)), pltpu.SemaphoreType.DMA((n_sem,))],
-        compiler_params=params(collective_id))(tokens, d_out, w_mix, *routing, w_gate, w_up, w_down)
+        compiler_params=params(collective_id))(tokens, d_out, w_mix, ids, gates, w_gate, w_up, w_down)
 
 
 def silu_parts(pre_gate):
@@ -427,9 +424,9 @@
 
 
 def split3(val):
-    hi = lax.reduce_precision(val, 8, 7)
+    hi = val.astype(BF16).astype(F32)
     rest = val - hi
-    mid = lax.reduce_precision(rest, 8, 7)
+    mid = rest.astype(BF16).astype(F32)
     return hi, mid, rest - mid
 
 
@@ -452,6 +449,12 @@
         val = 1.0 if values is None else jnp.broadcast_to(values[e:e + 1], slots.shape)
         blocks.append(jnp.where(mask, val, 0.0))
     return jnp.concatenate(blocks, axis=0)
+
+
+def unit(size):
+    row = lax.broadcasted_iota(jnp.int32, (size, size), 0)
+    col = lax.broadcasted_iota(jnp.int32, (size, size), 1)
+    return jnp.where(row == col, 1.0, 0.0).astype(BF16)
 
 
 def nn(a, b):
@@ -664,9 +667,9 @@
             both = jnp.concatenate([lo, hi], axis=1)
             return both[0], both[1], jnp.swapaxes(both[2], 1, 2)
 
-        routing = [jnp.swapaxes(expert_ids, 1, 2).astype(F32)] + list(split3(jnp.swapaxes(gate_vals, 1, 2)))
-        tok_all, route, w_first, own_top, u_act = open_line(tokens.T, d_out.T, w_mix, routing, w_gate, w_up,
-                                                            jnp.swapaxes(w_down, 2, 3), 1)
+        tok_all, route, w_first, own_top, u_act = open_line(
+            tokens.T, d_out.T, w_mix, jnp.swapaxes(expert_ids, 1, 2), jnp.swapaxes(gate_vals, 1, 2),
+            w_gate, w_up, jnp.swapaxes(w_down, 2, 3), 1)
         w_top = lax.all_gather(own_top.reshape(3 * n_half * d_model, ff), ('y', 'x'), axis=0, tiled=False)
         w_top = w_top.reshape(16, 3, n_half, d_model, ff)
 
@@ -690,7 +693,7 @@
         d_tokens, layer_out, mix_out = close_line(part_v, d_y, w_mix[0], tokens, mix_top, part_y, u_top, 4)
         grad_top, d_tokens = lax.optimization_barrier((grad_top, d_tokens))
         grads = [finish_grads(grad_low), finish_grads(grad_top)]
-        return (layer_out, d_tokens, mix_out) + tuple(jnp.stack([g[k] for g in grads]) for k in range(3))
+        return (layer_out.T, d_tokens.T, mix_out) + tuple(jnp.stack([g[k] for g in grads]) for k in range(3))
 
     return jax.shard_map(device_body, mesh=m4,
                          in_specs=(tok_spec, tok_spec, route_spec, route_spec, whole_spec,

time: 395 us -> 390 us (0.987)
  transfers between devices with their start and end apart: 5 -> 5, of which waited for: 2 -> 3; matrix products, arithmetic and copies ran while one was open for 2% -> 1% of each run, Pallas kernels for 63% -> 64%
where the time goes in v4:
time: 390 us
  Pallas kernels  340 us (87%)
  waiting for transfers between devices  21.1 us (5%)
  between operations  13.8 us (4%)
  local copies, waits for them, and re-layouts  6.57 us (2%)
  other arithmetic  4.74 us (1%)
    pallas_call x2, Pallas kernels, pass_line(): pl.pallas_call(functools.partial(pass_kernel, transpose, want_all), name=...  83.7 us
    pallas_call x1, Pallas kernels, close_line(): pl.pallas_call(close_kernel, name='close_line', out_shape=[block, block,...  74.2 us
    pallas_call x1, Pallas kernels, open_line(): pl.pallas_call(functools.partial(open_kernel, n_chip), name='open_line',...  71.5 us
    pallas_call x4, Pallas kernels, expert_combine(): local_call(functools.partial(combine_kernel, len(lefts)), n_mine, jax.Sha...  56.3 us
    pallas_call x1, Pallas kernels, expert_top(): local_call(top_kernel, n_mine, [jax.ShapeDtypeStruct(weights.shape, BF16)...  18.6 us
    pallas_call x1, Pallas kernels, expert_backward(): local_call(backward_kernel, n_mine, [jax.ShapeDtypeStruct(weights.shape,...  17.7 us
    reduce_scatter x2, waiting for transfers between devices, scatter_grads(): lax.psum_scatter(pack.reshape(16 * 3 * n_half * d_model, ff), ('y', 'x'),...  11.6 us
    pallas_call x1, Pallas kernels, expert_forward(): local_call(forward_kernel, n_mine, [per_slot(n_mine, width, BF16), per_sl...  9.84 us
  transfers between devices with their start and end apart: 5, of which 3 were waited for; matrix products, arithmetic and copies ran while one was open for 1% of the time, Pallas kernels for 64%

profile of v4, /device:TPU:1, one launch (start us, length us, event | category | flops | bytes accessed | tf_op | source)
XLA Modules:
  0.0 389.5 jit_solution(572429855538507368)
XLA Ops:
  7.2 71.5 %open_line.1 = (bf16[8,512,448]{2,1,0:T(8,128)(2,1)}, f32[2,4,8,32,256]{4,3,2,1,0:T(8,128)}, bf16[16,3,2,448,128]{4,3,2,1,0:T(8,128)(2,1)}, bf16[3,2,448,128]{3,2,1,0:T(8,128)(2,1)}, bf16[256,448]{1,0:T(8,128)(2,1)}) custom-call(bf16[448,256]{1,0:T(8,128)(2,1)} %bitcast.43, bf16[448,256]{1,0:T(8,128)(2,1)} %bitcast.42, bf16[2,448,448]{2,1,0:T(8,128)(2,1)} %w_mix.1, ...), custom_call_target="tpu_custom_call" | custom-call | tf_op jit(solution)/shard_map/open_line/pallas_call | solution.py:407
  78.8 9.8 %shard_map.127 = (bf16[32,192,448]{2,1,0:T(8,128)(2,1)}, f32[32,192,128]{2,1,0:T(8,128)}, f32[32,192,128]{2,1,0:T(8,128)}, bf16[32,192,128]{2,1,0:T(8,128)(2,1)}) custom-call(f32[2,4,8,32,256]{4,3,2,1,0:T(8,128)} %get-tuple-element.40.pos.hi.mid.lo, bf16[8,512,448]{2,1,0:T(8,128)(2,1)} %get-tuple-element.41.u_all.dy_all, ...), custom_call_target="tpu_custom_call" | custom-call | tf_op jit(solution)/shard_map/pallas_call | solution.py:592
  88.6 13.6 %shard_map.128.part = f32[8,256,448]{2,1,0:T(8,128)} custom-call(f32[2,4,8,32,256]{4,3,2,1,0:T(8,128)} %get-tuple-element.40.pos.hi.mid.lo, f32[2,4,8,32,256]{4,3,2,1,0:T(8,128)} %get-tuple-element.40.pos.hi.mid.lo, f32[2,4,8,32,256]{4,3,2,1,0:T(8,128)} %get-tuple-element.40.pos.hi.mid.lo, f32[2,4,8,32,256]{4,3,2,1,0:T(8,128)} %get-tuple-element.40.pos.hi.mid.lo, ...), custom_call_target="tpu_custom_call" | custom-call | tf_op jit(solution)/shard_map/pallas_call | solution.py:634
  102.2 1.0 slice_bitcast_fusion
  103.2 41.7 %pass_line.2 = (bf16[256,448]{1,0:T(8,128)(2,1)}, bf16[256,448]{1,0:T(8,128)(2,1)}, bf16[8,256,448]{2,1,0:T(8,128)(2,1)}) custom-call(f32[8,256,448]{2,1,0:T(8,128)} %shard_map.128.part, bf16[256,448]{1,0:T(8,128)(2,1)} %get-tuple-element.44.base, bf16[448,448]{1,0:T(8,128)(2,1)} %get-tuple-element.83.w_mix), custom_call_target="tpu_custom_call" | custom-call | tf_op jit(solution)/shard_map/pass_line/pallas_call | solution.py:154
  144.9 8.3 %shard_map.129 = (bf16[32,192,448]{2,1,0:T(8,128)(2,1)}, bf16[32,192,448]{2,1,0:T(8,128)(2,1)}) custom-call(f32[2,4,8,32,256]{4,3,2,1,0:T(8,128)} %get-tuple-element.40.pos.hi.mid.lo, f32[2,4,8,32,256]{4,3,2,1,0:T(8,128)} %get-tuple-element.40.pos.hi.mid.lo, f32[2,4,8,32,256]{4,3,2,1,0:T(8,128)} %get-tuple-element.40.pos.hi.mid.lo, ...), custom_call_target="tpu_custom_call" | custom-call | tf_op jit(solution)/shard_map/pallas_call | solution.py:614
  153.2 7.4 %all-gather.2.cloned.1.call-done = bf16[16,2688,128]{2,1,0:T(8,128)(2,1)} async-done(((bf16[1,2688,128]{2,1,0:T(8,128)(2,1)}), bf16[16,2688,128]{2,1,0:T(8,128)(2,1)}) %all-gather.2.cloned.1.call-update) | async-done | bytes 11010064 | tf_op jit(solution)/shard_map/all_gather | solution.py:673
  160.6 18.6 %shard_map.130 = (bf16[16,3,2,448,128]{4,3,2,1,0:T(8,128)(2,1)}, bf16[32,192,128]{2,1,0:T(8,128)(2,1)}, bf16[32,192,128]{2,1,0:T(8,128)(2,1)}, bf16[32,192,128]{2,1,0:T(8,128)(2,1)}) custom-call(bf16[32,192,448]{2,1,0:T(8,128)(2,1)} %get-tuple-element.47.recv, bf16[32,192,448]{2,1,0:T(8,128)(2,1)} %get-tuple-element.48.grad_in, ...), custom_call_target="tpu_custom_call" | custom-call | tf_op jit(solution)/shard_map/pallas_call | solution.py:623
  180.9 14.6 %shard_map.131.part = f32[8,256,448]{2,1,0:T(8,128)} custom-call(f32[2,4,8,32,256]{4,3,2,1,0:T(8,128)} %get-tuple-element.40.pos.hi.mid.lo, f32[2,4,8,32,256]{4,3,2,1,0:T(8,128)} %get-tuple-element.40.pos.hi.mid.lo, f32[2,4,8,32,256]{4,3,2,1,0:T(8,128)} %get-tuple-element.40.pos.hi.mid.lo, f32[2,4,8,32,256]{4,3,2,1,0:T(8,128)} %get-tuple-element.40.pos.hi.mid.lo, ...), custom_call_target="tpu_custom_call" | custom-call | tf_op jit(solution)/shard_map/pallas_call | solution.py:634
  195.6 42.0 %pass_line.3 = (bf16[256,448]{1,0:T(8,128)(2,1)}, bf16[256,448]{1,0:T(8,128)(2,1)}, bf16[8,256,448]{2,1,0:T(8,128)(2,1)}) custom-call(f32[8,256,448]{2,1,0:T(8,128)} %shard_map.131.part, bf16[256,448]{1,0:T(8,128)(2,1)} %copy.16.base, bf16[448,448]{1,0:T(8,128)(2,1)} %get-tuple-element.83.w_mix), custom_call_target="tpu_custom_call" | custom-call | tf_op jit(solution)/shard_map/pass_line/pallas_call | solution.py:154
  237.6 17.7 %shard_map.132 = (bf16[16,3,2,448,128]{4,3,2,1,0:T(8,128)(2,1)}, bf16[32,192,128]{2,1,0:T(8,128)(2,1)}, bf16[32,192,128]{2,1,0:T(8,128)(2,1)}) custom-call(f32[2,4,8,32,256]{4,3,2,1,0:T(8,128)} %get-tuple-element.40.pos.hi.mid.lo, f32[2,4,8,32,256]{4,3,2,1,0:T(8,128)} %get-tuple-element.40.pos.hi.mid.lo, ...), custom_call_target="tpu_custom_call" | custom-call | tf_op jit(solution)/shard_map/pallas_call | solution.py:602
  255.3 0.9 copy-done.3
  257.1 14.8 %shard_map.133.part_v = f32[8,256,448]{2,1,0:T(8,128)} custom-call(f32[2,4,8,32,256]{4,3,2,1,0:T(8,128)} %get-tuple-element.40.pos.hi.mid.lo, f32[2,4,8,32,256]{4,3,2,1,0:T(8,128)} %get-tuple-element.40.pos.hi.mid.lo, f32[2,4,8,32,256]{4,3,2,1,0:T(8,128)} %get-tuple-element.40.pos.hi.mid.lo, f32[2,4,8,32,256]{4,3,2,1,0:T(8,128)} %get-tuple-element.40.pos.hi.mid.lo, ...), custom_call_target="tpu_custom_call" | custom-call | tf_op jit(solution)/shard_map/pallas_call | solution.py:634
  271.8 13.3 %shard_map.134.part_y = f32[8,256,448]{2,1,0:T(8,128)} custom-call(f32[2,4,8,32,256]{4,3,2,1,0:T(8,128)} %get-tuple-element.40.pos.hi.mid.lo, f32[2,4,8,32,256]{4,3,2,1,0:T(8,128)} %get-tuple-element.40.pos.hi.mid.lo, f32[2,4,8,32,256]{4,3,2,1,0:T(8,128)} %get-tuple-element.40.pos.hi.mid.lo, f32[2,4,8,32,256]{4,3,2,1,0:T(8,128)} %get-tuple-element.40.pos.hi.mid.lo, ...), custom_call_target="tpu_custom_call" | custom-call | tf_op jit(solution)/shard_map/pallas_call | solution.py:634
  285.1 1.1 convolution_convert_fusion.mix_top
  286.2 74.2 %close_line.1 = (bf16[448,256]{1,0:T(8,128)(2,1)}, bf16[448,256]{1,0:T(8,128)(2,1)}, bf16[2,448,448]{2,1,0:T(8,128)(2,1)}) custom-call(f32[8,256,448]{2,1,0:T(8,128)} %shard_map.133.part_v, bf16[256,448]{1,0:T(8,128)(2,1)} %get-tuple-element.60.base_v, bf16[448,448]{1,0:T(8,128)(2,1)} %get-tuple-element.82.w_mix, bf16[256,448]{1,0:T(8,128)(2,1)} %copy.17.x_in, ...), custom_call_target="tpu_custom_call" | custom-call | tf_op jit(solution)/shard_map/close_line/pallas_call | solution.py:252
  360.7 11.6 %reduce-scatter.5.cloned.1.call-done = bf16[2688,128]{1,0:T(8,128)(2,1)} async-done(((bf16[43008,128]{1,0:T(8,128)(2,1)}), bf16[2688,128]{1,0:T(8,128)(2,1)}) %reduce-scatter.5.cloned.1.call-update) | async-done | bytes 688144 | tf_op jit(solution)/shard_map/reduce_scatter | solution.py:659
  372.3 1.7 collective-permute-start
  374.0 2.0 collective-permute-done
  375.9 1.5 broadcast_select_fusion
  377.7 1.0 pad_maximum_fusion.2
  378.7 1.0 pad_maximum_fusion
  379.7 1.0 pad_maximum_fusion.1
  382.1 0.9 copy.23
  (30 shorter events, 4.6 us)
Async XLA Ops:
  7.2 153.4 %all-gather.2.cloned.1.call-start = ((), (), s32[]{:S(2)}) async-start(), calls=%async_computation.2 | async-start | bytes 11698176 | tf_op jit(solution)/shard_map/all_gather | solution.py:673
  78.7 281.7 %reduce-scatter.3.cloned.1.call-start = ((), (), s32[]{:S(2)}) async-start(), calls=%async_computation.3 | async-start | bytes 11698176 | tf_op jit(solution)/shard_map/reduce_scatter | solution.py:659
  88.6 13.6 %copy-start = (bf16[2,448,448]{2,1,0:T(8,128)(2,1)S(1)}, bf16[2,448,448]{2,1,0:T(8,128)(2,1)}, u32[]{:S(2)}) copy-start(bf16[2,448,448]{2,1,0:T(8,128)(2,1)} %w_mix.1) | copy-start | bytes 2408452
  179.2 0.9 copy-start.2
  179.2 193.1 %reduce-scatter.5.cloned.1.call-start = ((), (), s32[]{:S(2)}) async-start(), calls=%async_computation.4 | async-start | bytes 11698176 | tf_op jit(solution)/shard_map/reduce_scatter | solution.py:659
  255.3 0.9 copy-start.3
  271.8 13.3 %copy-start.4 = (bf16[256,448]{1,0:T(8,128)(2,1)S(1)}, bf16[256,448]{1,0:T(8,128)(2,1)}, u32[]{:S(2)}) copy-start(bf16[256,448]{1,0:T(8,128)(2,1)} %get-tuple-element.61) | copy-start | bytes 688132
  271.8 13.3 %copy-start.5 = (bf16[256,448]{1,0:T(8,128)(2,1)S(1)}, bf16[256,448]{1,0:T(8,128)(2,1)}, u32[]{:S(2)}) copy-start(bf16[256,448]{1,0:T(8,128)(2,1)} %get-tuple-element.62) | copy-start | bytes 688132
  360.5 13.5 %collective-permute-start.1 = (bf16[2688,128]{1,0:T(8,128)(2,1)}, bf16[2688,128]{1,0:T(8,128)(2,1)S(1)}, u32[]{:S(2)}, u32[]{:S(2)}) collective-permute-start(bf16[2688,128]{1,0:T(8,128)(2,1)} %reduce-scatter.3.cloned.1.call-done), channel_id=1, source_target_pairs={{0,1},{1,0},{2,3},{3,2},{4,5},{5,4},{6,7},{7,6},{8,9},{9,8},{10,11... | collective-permute-start | bytes 2064392 | tf_op jit(solution)/shard_map/ppermute | solution.py:664
  372.3 3.7 collective-permute-start
  378.7 2.0 copy-start.7
  378.7 2.7 copy-start.6
  378.7 3.4 copy-start.1
Sparse Core Ops, SparseCore 0:
  78.9 81.6 all-gather.1
  179.3 89.6 reduce-scatter.2
  272.5 99.7 reduce-scatter.4
